TPU v7x, 32 devices: a whole 2x2x4 slice. The times are simulated.
32 devices in a mesh: groups: 2 (over y), expert: 4 (over x, core), cuts: 4 (over z).
Axes of the slice: x: 2, y: 2, z: 4, core: 2. Of those that a mesh axis runs over, the one named last changes fastest.
Arguments:
- tokens: bfloat16 [4096, 2048], P(('groups', 'expert')), parts along dimension 0, may hold values from -6 to 6
- route: int32 [4096, 1], P(('groups', 'expert')), parts along dimension 0, may hold values from 0 to 3; in each aligned block of 512 rows (0 to 511, 512 to 1023, ...) at most 192 rows name the same one
- gate_prob: float32 [4096], P(('groups', 'expert')), parts along dimension 0, may hold values from 0.2 to 1
- norm_gain: float32 [2048], replicated, may hold values from 0.5 to 1.5
- dense_in: bfloat16 [2048, 8192], P('expert', 'cuts'), may hold values from -0.125 to 0.125
- dense_out: bfloat16 [8192, 2048], P('cuts', 'expert'), may hold values from -0.0625 to 0.0625
- expert_in: bfloat16 [4, 2048, 8192], P('expert', None, 'cuts'), may hold values from -0.125 to 0.125
- expert_out: bfloat16 [4, 8192, 2048], P('expert', 'cuts'), may hold values from -0.0625 to 0.0625
Outputs:
- layer_out: bfloat16 [4096, 2048], P(('groups', 'expert'), 'cuts'), parts along dimension 0
There are 2 independent parts, one for each index of `groups`. A program takes and returns all parts, laid end to end along the dimension named above; an argument that names none is the same for every part. Nothing has to cross between parts.
Inputs may be any that keep to these rules, and one draw needn't show every extreme that they name: `route`: within the rows of one device (aligned blocks of 512 rows) no expert is named by more than 192 rows; in some blocks one expert is named by exactly 192 rows.
All inputs are finite; a program needn't handle non-finite values.
Results may differ from a plain program's by a relative error of at most 0.0095.
Values may be sent and summed in bfloat16 or wider, within the bound.
A program may use at most 128 MiB of HBM per device.

v0:
```python
import functools

import jax
import jax.numpy as jnp
from jax import lax
from jax.experimental import pallas as pl
from jax.experimental.pallas import tpu as pltpu
from jax.sharding import PartitionSpec as P

SUBS = (4, 4)
WINDOW = 3
EARLY = 1


def kernel(G, E, Z, cap, tokens, route, gate, gain, din, dout, ein_h, eout_h, out,
           win, wout, ein, eout, tok, normed, disp, arrived, hbuf, pe, rpe, pd, rpd, ret, rret, base,
           loc, own_s, own_r, disp_s, disp_r, wx_s, wx_r, wy_s, wy_r, wp_s, wp_r,
           ze_s, ze_r, zd_s, zd_r, ret_s, ret_r):
    f32, bf16 = jnp.float32, jnp.bfloat16
    T, D = tok.shape
    F = ein.shape[1]
    De = D // E
    share = D // Z
    C = E // 2
    pair = 2 * cap
    tn = min(256, share)
    g, e, z = lax.axis_index("groups"), lax.axis_index("expert"), lax.axis_index("cuts")
    chip, core = e // 2, lax.rem(e, 2)
    partner = chip * 2 + 1 - core

    def remote(src, dst, send, recv, gg=None, ee=None, zz=None):
        return pltpu.make_async_remote_copy(
            src_ref=src, dst_ref=dst, send_sem=send, recv_sem=recv,
            device_id={
                "groups": g if gg is None else gg,
                "expert": e if ee is None else ee,
                "cuts": z if zz is None else zz,
            },
            device_id_type=pl.DeviceIdType.MESH,
        )

    def expert_at(kc, j):
        other = lax.rem(chip + kc + C, C)
        return other * 2 + (core if j == 0 else 1 - core)

    barrier = pltpu.get_barrier_semaphore()
    for k in range(1, E):
        pl.semaphore_signal(barrier, inc=1, device_id={"groups": g, "expert": lax.rem(e + k, E), "cuts": z},
                            device_id_type=pl.DeviceIdType.MESH)
    for k in range(1, Z):
        pl.semaphore_signal(barrier, inc=1, device_id={"groups": g, "expert": e, "cuts": lax.rem(z + k, Z)},
                            device_id_type=pl.DeviceIdType.MESH)
    for k in range(1, G):
        pl.semaphore_signal(barrier, inc=1, device_id={"groups": lax.rem(g + k, G), "expert": e, "cuts": z},
                            device_id_type=pl.DeviceIdType.MESH)

    my_rows = pl.ds(pl.multiple_of(e * De, De), De)
    locals_ = [
        pltpu.make_async_copy(tokens, tok, loc.at[0]),
        pltpu.make_async_copy(ein_h.at[0], ein, loc.at[1]),
        pltpu.make_async_copy(eout_h.at[0], eout, loc.at[2]),
        pltpu.make_async_copy(din, win.at[my_rows, :], loc.at[3]),
        pltpu.make_async_copy(dout, wout.at[:, my_rows], loc.at[4]),
    ]
    for copy in locals_:
        copy.start()
    pl.semaphore_wait(barrier, (E - 1) + (Z - 1) + (G - 1))

    own_copies = [
        remote(din, win.at[my_rows, :], own_s.at[0], own_r.at[0], ee=partner),
        remote(dout, wout.at[:, my_rows], own_s.at[1], own_r.at[1], ee=partner),
    ]

    def weight(m, owner, p, s):
        if m == 0:
            n = De // G // SUBS[m]
            return win.at[pl.ds(pl.multiple_of(owner * De + p * (De // G) + s * n, n), n), :]
        n = F // G // SUBS[m]
        return wout.at[pl.ds(pl.multiple_of(p * (F // G) + s * n, n), n),
                       pl.ds(pl.multiple_of(owner * De, De), De)]

    def weight_source(m, p, s):
        ref, rows = (din, De) if m == 0 else (dout, F)
        n = rows // G // SUBS[m]
        return ref.at[pl.ds(pl.multiple_of(p * (rows // G) + s * n, n), n), :]

    def x_copy(m, kc, s):
        return remote(weight_source(m, g, s), weight(m, e, g, s), wx_s.at[m, kc, s], wx_r.at[m, kc, s],
                      ee=expert_at(kc, 0))

    def y_copy(m, kc, s, dg):
        w = weight(m, expert_at(-kc, 0), g, s)
        return remote(w, w, wy_s.at[m, kc, s, dg], wy_r.at[m, kc, s, dg], gg=lax.rem(g + dg, G))

    def p_copy(m, kc, s, dg):
        w = weight(m, expert_at(-kc, 0), lax.rem(g - dg + G, G), s)
        return remote(w, w, wp_s.at[m, kc, s, dg], wp_r.at[m, kc, s, dg], ee=partner)

    steps = [(m, s) for m in range(2) for s in range(SUBS[m])]
    issued, taken, relayed = [0], [0], [0]

    def issue(upto):
        while issued[0] < min(upto, len(steps)):
            m, s = steps[issued[0]]
            for kc in range(1, C):
                x_copy(m, kc, s).start()
            issued[0] += 1

    def relay():
        m, s = steps[relayed[0]]
        for kc in range(1, C):
            for dg in range(1, G):
                y_copy(m, kc, s, dg).wait_recv()
                p_copy(m, kc, s, dg).start()
        relayed[0] += 1

    def take(upto):
        while taken[0] < min(upto, len(steps)):
            m, s = steps[taken[0]]
            for kc in range(1, C):
                x_copy(m, kc, s).wait_recv()
            if taken[0] >= EARLY:
                issue(taken[0] + 1 + WINDOW)
            for kc in range(1, C):
                for dg in range(1, G):
                    y_copy(m, kc, s, dg).start()
                p_copy(m, kc, s, 0).start()
            if relayed[0] < taken[0]:
                relay()
            taken[0] += 1

    issue(EARLY)
    locals_[0].wait()

    nrow = min(64, T)

    def norm_step(i, carry):
        rows = pl.ds(pl.multiple_of(i * nrow, nrow), nrow)
        x = tok[rows, :].astype(f32)
        ms = jnp.mean(x * x, axis=-1, keepdims=True)
        normed[rows, :] = (x * lax.rsqrt(ms + 1e-06) * gain[...]).astype(bf16)
        return carry

    lax.fori_loop(0, T // nrow, norm_step, 0)

    picked = route[...]
    one_hot = (lax.broadcasted_iota(jnp.int32, (T, 128), 1) == picked).astype(f32)
    lower = (lax.broadcasted_iota(jnp.int32, (T, T), 1) < lax.broadcasted_iota(jnp.int32, (T, T), 0))
    before = jnp.dot(lower.astype(f32).astype(bf16), one_hot.astype(bf16), preferred_element_type=f32)
    position = jnp.sum(before * one_hot, axis=1, keepdims=True)
    slot_col = picked.astype(f32) * float(cap) + position
    slot_row = jnp.transpose(jnp.broadcast_to(slot_col, (T, 128)))[0:1, :]

    def fill(q, dst):
        dest = expert_at(q // 2, q % 2)
        wanted = slot_row - (dest * cap).astype(f32)
        pick = (lax.broadcasted_iota(jnp.int32, (cap, T), 0).astype(f32) == wanted).astype(f32).astype(bf16)
        dn = min(512, D)

        def step(i, carry):
            cols = pl.ds(pl.multiple_of(i * dn, dn), dn)
            dst[q * cap:(q + 1) * cap, cols] = jnp.dot(
                pick, normed[:, cols], preferred_element_type=f32).astype(bf16)
            return carry

        lax.fori_loop(0, D // dn, step, 0)

    def disp_copy(q):
        return remote(disp.at[pl.ds(q * cap, cap), :], arrived.at[pl.ds(q * cap, cap), :],
                      disp_s.at[q], disp_r.at[q], ee=expert_at(q // 2, q % 2))

    order = list(range(2, E)) + [1]
    pending = None
    for q in order:
        fill(q, disp)
        if pending is not None:
            disp_copy(pending).start()
        pending = q
    fill(0, arrived)
    disp_copy(pending).start()

    for copy in own_copies:
        copy.start()

    def ze_copy(kc, r):
        rows = pl.ds(kc * pair, pair)
        return remote(pe.at[r, rows, :], rpe.at[r, rows, :], ze_s.at[kc, r], ze_r.at[kc, r],
                      zz=lax.rem(z + r, Z))

    halfrows = T // 2

    def zd_copy(d, slot, c, to):
        rows = pl.ds(c * halfrows, halfrows)
        return remote(pd.at[d, rows, :], rpd.at[slot, rows, :], zd_s.at[d, c], zd_r.at[slot, c], zz=to)

    def back_slot(d, to):
        return Z if d == to else d

    def hidden(load, rows, w, lo=0, hi=None):
        def step(i, carry):
            cols = pl.ds(pl.multiple_of(i * 256, 256), 256)
            acc = jnp.dot(load(), w[:, cols], preferred_element_type=f32)
            hbuf[0:rows, cols] = jax.nn.gelu(acc).astype(bf16)
            return carry

        lax.fori_loop(lo, F // 256 if hi is None else hi, step, 0)

    def partials(rows, w, store, send):
        late = None
        for r in list(range(Z - 1, 0, -1)) + [0]:
            base = lax.rem(z + r, Z) * share

            def step(i, carry):
                cols = pl.ds(pl.multiple_of(base + i * tn, tn), tn)
                acc = jnp.dot(hbuf[0:rows, :], w[:, cols], preferred_element_type=f32)
                store(r, pl.ds(pl.multiple_of(i * tn, tn), tn), acc.astype(bf16))
                return carry

            lax.fori_loop(0, share // tn, step, 0)
            if late is not None:
                send(late).start()
            late = r

    locals_[1].wait()
    locals_[2].wait()
    for kc in range(C):
        for q in (2 * kc, 2 * kc + 1):
            if q:
                disp_copy(q).wait_recv()
        if kc == C - 1:
            issue(EARLY + WINDOW)
        lo = kc * pair
        hidden(lambda: arrived[lo:lo + pair, :], pair, ein)

        def store(r, cols, value):
            pe[r, lo:lo + pair, cols] = value

        partials(pair, eout, store, lambda r: ze_copy(kc, r))
        if kc == 0:
            take(EARLY)

    def collect(m):
        locals_[3 + m].wait()
        own_copies[m].wait_recv()
        for s in range(SUBS[m]):
            for kc in range(1, C):
                for dg in range(G):
                    p_copy(m, kc, s, dg).wait_recv()

    first = SUBS[0]
    take(first + 1)
    while relayed[0] < first:
        relay()
    collect(0)
    blocks = F // 256
    for part in range(4):
        hidden(lambda: normed[...], T, win, part * blocks // 4, (part + 1) * blocks // 4)
        take(first + 2 + part)
    take(len(steps))
    while relayed[0] < len(steps):
        relay()
    collect(1)

    upper = (2 * z) // Z
    for i in range(Z):
        d = (1 - upper) * (Z - 1 - i) + upper * i

        def dense_step(k, carry):
            cols = pl.ds(pl.multiple_of(d * share + k * tn, tn), tn)
            acc = jnp.dot(hbuf[0:T, :], wout[:, cols], preferred_element_type=f32)
            pd[d, :, pl.ds(pl.multiple_of(k * tn, tn), tn)] = acc.astype(bf16)
            return carry

        lax.fori_loop(0, share // tn, dense_step, 0)
        if i < Z - 1:
            @pl.when(z == 0)
            def _():
                for c in range(2):
                    zd_copy(Z - 1 - i, Z - 1 - i, c, 1).start()

            @pl.when(z == Z - 1)
            def _():
                for c in range(2):
                    zd_copy(i, back_slot(i, Z - 2), c, Z - 2).start()

    def ret_copy(q):
        return remote(ret.at[pl.ds(q * cap, cap), :], rret.at[pl.ds(q * cap, cap), :],
                      ret_s.at[q], ret_r.at[q], ee=expert_at(-(q // 2), q % 2))

    for kc in list(range(1, C)) + [0]:
        lo = kc * pair
        for r in range(1, Z):
            ze_copy(kc, r).wait_recv()
        for q in (2 * kc + 1, 2 * kc):
            rows = slice(q * cap, (q + 1) * cap)
            total = pe[0, rows, :].astype(f32)
            for r in range(1, Z):
                total = total + rpe[r, rows, :].astype(f32)
            if q:
                ret[rows, :] = total.astype(bf16)
            else:
                rret[rows, :] = total.astype(bf16)
        for q in (2 * kc, 2 * kc + 1):
            if q:
                ret_copy(q).start()

    def add_arrived(d, c):
        rows = slice(c * halfrows, (c + 1) * halfrows)
        pd[d, rows, :] = (pd[d, rows, :].astype(f32) + rpd[d, rows, :].astype(f32)).astype(bf16)

    trow = min(128, T)
    residual = pl.ds(pl.multiple_of(z * share, share), share)

    def combine_experts():
        for q in range(1, E):
            ret_copy(q).wait_recv()
        for i in range(T // trow):
            rows = slice(i * trow, (i + 1) * trow)
            res = jnp.zeros((trow, share), f32)
            for q in range(E):
                wanted = slot_col[rows, :] - (expert_at(q // 2, q % 2) * cap).astype(f32)
                pick = (lax.broadcasted_iota(jnp.int32, (trow, cap), 1).astype(f32) == wanted)
                res = res + jnp.dot(pick.astype(f32).astype(bf16), rret[q * cap:(q + 1) * cap, :],
                                    preferred_element_type=f32)
            base[rows, :] = tok[rows, residual].astype(f32) + gate[rows, :] * res

    above, below = lax.rem(z + 1, Z), lax.rem(z + Z - 1, Z)

    def pass_up(d, c):
        @pl.when((z > 0) & (z < d))
        def _():
            zd_copy(d, d, c, above).wait_recv()
            add_arrived(d, c)
            zd_copy(d, d, c, above).start()

    def pass_down(d, c):
        for slot, near in ((d, z > d + 1), (Z, z == d + 1)):
            @pl.when((z < Z - 1) & near)
            def _():
                zd_copy(d, d, c, below).wait_recv()
                add_arrived(d, c)
                zd_copy(d, slot, c, below).start()

    for t in range(Z - 1):
        @pl.when(upper == 0)
        def _():
            for c in range(2):
                pass_up(Z - 1 - t, c)
            for c in range(2):
                pass_down(t, c)

        @pl.when(upper == 1)
        def _():
            for c in range(2):
                pass_down(t, c)
            for c in range(2):
                pass_up(Z - 1 - t, c)

        if t == 0:
            combine_experts()

    @pl.when(z == 0)
    def _():
        rpd[0] = jnp.zeros((T, share), bf16)

    @pl.when(z == Z - 1)
    def _():
        rpd[Z] = jnp.zeros((T, share), bf16)

    for c in range(2):
        @pl.when(z > 0)
        def _():
            zd_copy(z, z, c, lax.rem(z + 1, Z)).wait_recv()

        @pl.when(z < Z - 1)
        def _():
            zd_copy(z, Z, c, lax.rem(z + 1, Z)).wait_recv()

    for i in range(T // trow):
        rows = slice(i * trow, (i + 1) * trow)
        dense = pd[z, rows, :].astype(f32) + rpd[z, rows, :].astype(f32) + rpd[Z, rows, :].astype(f32)
        out[rows, :] = (base[rows, :] + dense).astype(bf16)

    for copy in own_copies:
        copy.wait_send()
    for q in range(1, E):
        disp_copy(q).wait_send()
        ret_copy(q).wait_send()
    for m in range(2):
        for s in range(SUBS[m]):
            for kc in range(1, C):
                x_copy(m, kc, s).wait_send()
                for dg in range(1, G):
                    y_copy(m, kc, s, dg).wait_send()
                for dg in range(G):
                    p_copy(m, kc, s, dg).wait_send()
    for r in range(1, Z):
        for kc in range(C):
            ze_copy(kc, r).wait_send()
    for d in range(Z):
        @pl.when(z != d)
        def _():
            for c in range(2):
                zd_copy(d, d, c, lax.rem(z + 1, Z)).wait_send()


def local(tokens, route, gate_prob, norm_gain, dense_in, dense_out, expert_in, expert_out):
    G, E, Z = lax.axis_size("groups"), lax.axis_size("expert"), lax.axis_size("cuts")
    T, D = tokens.shape
    F = dense_in.shape[1]
    share = D // Z
    cap = max(2, 3 * T // (2 * E))
    C = E // 2
    bf16 = jnp.bfloat16
    any_, vmem = pl.BlockSpec(memory_space=pl.ANY), pl.BlockSpec(memory_space=pltpu.VMEM)
    dma = pltpu.SemaphoreType.DMA
    return pl.pallas_call(
        functools.partial(kernel, G, E, Z, cap),
        out_shape=jax.ShapeDtypeStruct((T, share), bf16),
        in_specs=[any_, vmem, vmem, vmem, any_, any_, any_, any_],
        out_specs=vmem,
        scratch_shapes=[
            pltpu.VMEM((D, F), bf16), pltpu.VMEM((F, D), bf16),
            pltpu.VMEM((D, F), bf16), pltpu.VMEM((F, D), bf16),
            pltpu.VMEM((T, D), bf16), pltpu.VMEM((T, D), bf16),
            pltpu.VMEM((E * cap, D), bf16), pltpu.VMEM((E * cap, D), bf16),
            pltpu.VMEM((max(T, 2 * cap), F), bf16),
            pltpu.VMEM((Z, E * cap, share), bf16), pltpu.VMEM((Z, E * cap, share), bf16),
            pltpu.VMEM((Z, T, share), bf16), pltpu.VMEM((Z + 1, T, share), bf16),
            pltpu.VMEM((E * cap, share), bf16), pltpu.VMEM((E * cap, share), bf16),
            pltpu.VMEM((T, share), jnp.float32),
            dma((5,)), dma((2,)), dma((2,)), dma((E,)), dma((E,)),
            dma((2, C, max(SUBS))), dma((2, C, max(SUBS))),
            dma((2, C, max(SUBS), G)), dma((2, C, max(SUBS), G)), dma((2, C, max(SUBS), G)), dma((2, C, max(SUBS), G)),
            dma((C, Z)), dma((C, Z)), dma((Z, 2)), dma((Z + 1, 2)), dma((E,)), dma((E,)),
        ],
        compiler_params=pltpu.CompilerParams(
            collective_id=0, has_side_effects=True, vmem_limit_bytes=67043328
        ),
    )(tokens, route, gate_prob[:, None], norm_gain[None, :], dense_in, dense_out, expert_in, expert_out)


def solution(mesh):
    return jax.shard_map(
        local,
        mesh=mesh,
        in_specs=(
            P(("groups", "expert"), None),
            P(("groups", "expert"), None),
            P(("groups", "expert")),
            P(),
            P("expert", "cuts"),
            P("cuts", "expert"),
            P("expert", None, "cuts"),
            P("expert", "cuts", None),
        ),
        out_specs=P(("groups", "expert"), "cuts"),
        check_vma=False,
    )
```

profile of v0, /device:TPU:2, one launch (start us, length us, event | category | flops | bytes accessed | tf_op | source)
XLA Modules:
  0.0 140.9 jit_solution(14794617653891997243)
XLA Ops:
  0.0 1.5 %copy.10.route = s32[512,1]{1,0:T(8,128)} copy(s32[512,1]{0,1:T(1,128)} %param.9) | data formatting | bytes 4096 | tf_op args[1]
  1.5 1.5 %copy.11.gate = f32[512,1]{1,0:T(8,128)} copy(f32[512,1]{0,1:T(1,128)} %bitcast.3) | data formatting | bytes 4096 | tf_op jit(solution)/shard_map/broadcast_in_dim | solution.py:440
  3.1 136.0 %shard_map.82 = bf16[512,512]{1,0:T(8,128)(2,1)} custom-call(bf16[512,2048]{1,0:T(8,128)(2,1)} %tokens.1, s32[512,1]{1,0:T(8,128)} %copy.10.route, f32[512,1]{1,0:T(8,128)} %copy.11.gate, f32[1,2048]{1,0:T(1,128)} %bitcast.2, bf16[512,2048]{1,0:T(8,128)(2,1)} %din.1, bf16[2048,512]{1,0:T(8,128)(2,1)} %dout.1, bf16[1,2048,2048]{2,1,0:T(8,128)(2,1)} %ein_h.1, ...), custom_call_target="tpu_custom_call" | custom-call | tf_op jit(solution)/shard_map/pallas_call | solution.py:417
  139.0 1.9 %copy.13 = bf16[512,512]{1,0:T(8,128)(2,1)} copy(bf16[512,512]{1,0:T(8,128)(2,1)} %shard_map.82) | data formatting | bytes 1048576
where the time goes:
time: 144 us; the launch traced here: 141 us
  Pallas kernels  136 us (94%)
  local copies, waits for them, and re-layouts  4.94 us (3%)
    pallas_call x1, Pallas kernels, local(): pl.pallas_call(functools.partial(kernel, G, E, Z, cap), out_shape=jax.Sha...  136 us
    unnamed x2, local copies, waits for them, and re-layouts  3.4 us

commit v1 on v0

v1 whole, which is shorter than its diff:
```python
import functools

import jax
import jax.numpy as jnp
from jax import lax
from jax.experimental import pallas as pl
from jax.experimental.pallas import tpu as pltpu
from jax.sharding import PartitionSpec as P

SUBS = (4, 4)
EARLY = 1


def kernel(G, E, Z, cap, nk, tokens, route, gate, gain, din, dout, ein_h, eout_h, out,
           win, wout, ein, eout, tok, normed, disp, dispq, arrived, hbuf, pown, psend, po, rpo, pd, rpd,
           ret, rret, base, pk,
           loc, own_s, own_r, d1_s, d1_r, dx_s, dx_r, ag_s, ag_r, pq_s, pq_r,
           wx_s, wx_r, wy_s, wy_r, wp_s, wp_r, zo_s, zo_r, zd_s, zd_r, ret_s, ret_r):
    f32, bf16 = jnp.float32, jnp.bfloat16
    T, D = tok.shape
    F = ein.shape[1]
    De = D // E
    share = D // Z
    C = E // 2
    wide = share // nk
    tn = min(256, wide)
    units = range(2, E)
    g, e, z = lax.axis_index("groups"), lax.axis_index("expert"), lax.axis_index("cuts")
    chip, core = e // 2, lax.rem(e, 2)
    partner = chip * 2 + 1 - core
    above, below = lax.rem(z + 1, Z), lax.rem(z + Z - 1, Z)
    upper = (2 * z) // Z

    def remote(src, dst, send, recv, gg=None, ee=None, zz=None):
        return pltpu.make_async_remote_copy(
            src_ref=src, dst_ref=dst, send_sem=send, recv_sem=recv,
            device_id={
                "groups": g if gg is None else gg,
                "expert": e if ee is None else ee,
                "cuts": z if zz is None else zz,
            },
            device_id_type=pl.DeviceIdType.MESH,
        )

    def when(condition):
        return pl.when(condition)

    def expert_at(kc, j):
        other = lax.rem(chip + kc + C, C)
        return other * 2 + (core if j == 0 else 1 - core)

    my_rows = pl.ds(pl.multiple_of(e * De, De), De)
    locals_ = [
        pltpu.make_async_copy(tokens, tok, loc.at[0]),
        pltpu.make_async_copy(ein_h.at[0], ein, loc.at[1]),
        pltpu.make_async_copy(eout_h.at[0], eout, loc.at[2]),
        pltpu.make_async_copy(din, win.at[my_rows, :], loc.at[3]),
        pltpu.make_async_copy(dout, wout.at[:, my_rows], loc.at[4]),
    ]
    locals_[0].start()

    barrier = pltpu.get_barrier_semaphore()
    for k in range(1, E):
        pl.semaphore_signal(barrier, inc=1, device_id={"groups": g, "expert": lax.rem(e + k, E), "cuts": z},
                            device_id_type=pl.DeviceIdType.MESH)
    for k in range(1, Z):
        pl.semaphore_signal(barrier, inc=1, device_id={"groups": g, "expert": e, "cuts": lax.rem(z + k, Z)},
                            device_id_type=pl.DeviceIdType.MESH)
    for k in range(1, G):
        pl.semaphore_signal(barrier, inc=1, device_id={"groups": lax.rem(g + k, G), "expert": e, "cuts": z},
                            device_id_type=pl.DeviceIdType.MESH)
    pl.semaphore_wait(barrier, (E - 1) + (Z - 1) + (G - 1))

    own_copies = [
        remote(din, win.at[my_rows, :], own_s.at[0], own_r.at[0], ee=partner),
        remote(dout, wout.at[:, my_rows], own_s.at[1], own_r.at[1], ee=partner),
    ]

    def block(m, p, s):
        if m == 0:
            n = De // G // SUBS[0]
            return p * (De // G) + s * n, n, 0, F
        per = SUBS[1] // nk
        n = F // G // per
        return p * (F // G) + (s % per) * n, n, (s // per) * (De // nk), De // nk

    def weight(m, owner, p, s):
        row, n, col, width = block(m, p, s)
        if m == 0:
            return win.at[pl.ds(pl.multiple_of(owner * De + row, n), n), :]
        return wout.at[pl.ds(pl.multiple_of(row, n), n),
                       pl.ds(pl.multiple_of(owner * De + col, width), width)]

    def weight_source(m, p, s):
        row, n, col, width = block(m, p, s)
        return (din, dout)[m].at[pl.ds(pl.multiple_of(row, n), n), pl.ds(col, width)]

    def x_copy(m, kc, s):
        return remote(weight_source(m, g, s), weight(m, e, g, s), wx_s.at[m, kc, s], wx_r.at[m, kc, s],
                      ee=expert_at(kc, 0))

    def y_copy(m, kc, s, dg):
        w = weight(m, expert_at(-kc, 0), g, s)
        return remote(w, w, wy_s.at[m, kc, s, dg], wy_r.at[m, kc, s, dg], gg=lax.rem(g + dg, G))

    def p_copy(m, kc, s, dg):
        w = weight(m, expert_at(-kc, 0), lax.rem(g - dg + G, G), s)
        return remote(w, w, wp_s.at[m, kc, s, dg], wp_r.at[m, kc, s, dg], ee=partner)

    steps = [(m, s) for m in range(2) for s in range(SUBS[m])]
    issued, taken, relayed = [0], [0], [0]

    def issue(upto):
        while issued[0] < min(upto, len(steps)):
            m, s = steps[issued[0]]
            for kc in range(1, C):
                x_copy(m, kc, s).start()
            issued[0] += 1

    def relay(upto):
        while relayed[0] < min(upto, taken[0]):
            m, s = steps[relayed[0]]
            for kc in range(1, C):
                for dg in range(1, G):
                    y_copy(m, kc, s, dg).wait_recv()
                    p_copy(m, kc, s, dg).start()
            relayed[0] += 1

    def take(upto):
        while taken[0] < min(upto, len(steps)):
            m, s = steps[taken[0]]
            for kc in range(1, C):
                x_copy(m, kc, s).wait_recv()
                for dg in range(1, G):
                    y_copy(m, kc, s, dg).start()
                p_copy(m, kc, s, 0).start()
            taken[0] += 1

    def collect(m, subs):
        for s in subs:
            for kc in range(1, C):
                for dg in range(G):
                    p_copy(m, kc, s, dg).wait_recv()

    issue(EARLY)
    locals_[0].wait()
    for copy in locals_[1:]:
        copy.start()

    nrow = min(64, T)

    def norm_step(i, carry):
        rows = pl.ds(pl.multiple_of(i * nrow, nrow), nrow)
        x = tok[rows, :].astype(f32)
        ms = jnp.mean(x * x, axis=-1, keepdims=True)
        normed[rows, :] = (x * lax.rsqrt(ms + 1e-06) * gain[...]).astype(bf16)
        return carry

    lax.fori_loop(0, T // nrow, norm_step, 0)

    picked = route[...]
    one_hot = (lax.broadcasted_iota(jnp.int32, (T, 128), 1) == picked).astype(f32)
    lower = (lax.broadcasted_iota(jnp.int32, (T, T), 1) < lax.broadcasted_iota(jnp.int32, (T, T), 0))
    before = jnp.dot(lower.astype(f32).astype(bf16), one_hot.astype(bf16), preferred_element_type=f32)
    position = jnp.sum(before * one_hot, axis=1, keepdims=True)
    slot_col = picked.astype(f32) * float(cap) + position
    slot_row = jnp.transpose(jnp.broadcast_to(slot_col, (T, 128)))[0:1, :]

    def slice_at(s):
        return pl.ds(pl.multiple_of(s * share, share), share)

    def picks(q):
        dest = expert_at(q // 2, q % 2)
        wanted = slot_row - (dest * cap).astype(f32)
        return (lax.broadcasted_iota(jnp.int32, (cap, T), 0).astype(f32) == wanted).astype(f32).astype(bf16)

    def fill_slice(q, x, s):
        disp[x, (q - 2) * cap:(q - 1) * cap, :] = jnp.dot(
            picks(q), normed[:, slice_at(s)], preferred_element_type=f32).astype(bf16)

    def fill(q, dst):
        pick = picks(q)
        dn = min(512, D)

        def step(i, carry):
            cols = pl.ds(pl.multiple_of(i * dn, dn), dn)
            dst[0:cap, cols] = jnp.dot(pick, normed[:, cols], preferred_element_type=f32).astype(bf16)
            return carry

        lax.fori_loop(0, D // dn, step, 0)

    ends = ((0, Z - 1), (Z - 1, 0))

    def dx_copy(q, x, s):
        return remote(disp.at[x, pl.ds((q - 2) * cap, cap), :], arrived.at[pl.ds(q * cap, cap), slice_at(s)],
                      dx_s.at[q, x], dx_r.at[q, x], ee=expert_at(q // 2, q % 2))

    d1_copy = remote(dispq, arrived.at[pl.ds(cap, cap), :], d1_s.at[0], d1_r.at[0], ee=partner)

    pending = None
    for q in units:
        fill_slice(q, 0, z)
        if pending is not None:
            dx_copy(pending, 0, z).start()
        pending = q
    for at, s in ends:
        @when(z == at)
        def _():
            for q in units:
                fill_slice(q, 1, s)
    if pending is not None:
        dx_copy(pending, 0, z).start()
    fill(1, dispq)
    for at, s in ends:
        @when(z == at)
        def _():
            for q in units:
                dx_copy(q, 1, s).start()
    issue(len(steps))
    fill(0, arrived)
    d1_copy.start()
    for copy in own_copies:
        copy.start()

    def hop(q, way, t, s):
        part = arrived.at[pl.ds(q * cap, cap), slice_at(s)]
        return remote(part, part, ag_s.at[q, way, t], ag_r.at[q, way, t], zz=below if way else above)

    def gather(q, t):
        if t == 0:
            dx_copy(q, 0, z).wait_recv()

        @when(z >= t)
        def _():
            if t > 0:
                hop(q, 0, t, z - t).wait_recv()
        if t < Z - 2:
            @when((z >= t) & (z < Z - 1))
            def _():
                hop(q, 0, t + 1, z - t).start()

        @when(z + t <= Z - 1)
        def _():
            if t > 0:
                hop(q, 1, t, z + t).wait_recv()
        if t < Z - 2:
            @when((z + t <= Z - 1) & (z > 0))
            def _():
                hop(q, 1, t + 1, z + t).start()

    def hidden(load, rows, w, lo=0, hi=None):
        def step(i, carry):
            cols = pl.ds(pl.multiple_of(i * 256, 256), 256)
            acc = jnp.dot(load(), w[:, cols], preferred_element_type=f32)
            hbuf[0:rows, cols] = jax.nn.gelu(acc).astype(bf16)
            return carry

        lax.fori_loop(lo, F // 256 if hi is None else hi, step, 0)

    blocks = F // 256

    def part_of(i, n):
        return i * blocks // n, (i + 1) * blocks // n

    pair = 2 * cap
    take(EARLY)
    col = lax.broadcasted_iota(jnp.int32, (T, pair), 1).astype(f32)
    here = slot_col - (e * cap).astype(f32)
    there = slot_col - (partner * cap).astype(f32) + float(cap)
    pk[...] = (((col == here) & (col < cap)) | ((col == there) & (col >= cap))).astype(f32).astype(bf16)

    locals_[1].wait()
    d1_copy.wait_recv()
    for i in range(4):
        hidden(lambda: arrived[0:pair, :], pair, ein, *part_of(i, 4))
        if i == 1:
            for q in units:
                gather(q, 0)

    locals_[2].wait()

    def own_step(i, carry):
        cols = pl.ds(pl.multiple_of(i * 256, 256), 256)
        acc = jnp.dot(hbuf[0:pair, :], eout[:, cols], preferred_element_type=f32).astype(bf16)
        pown[0:cap, cols] = acc[0:cap, :]
        psend[:, cols] = acc[cap:pair, :]
        return carry

    own_blocks = D // 256
    lax.fori_loop(0, own_blocks // 2, own_step, 0)
    if Z > 2:
        for q in units:
            gather(q, 1)
    relay(EARLY)
    lax.fori_loop(own_blocks // 2, own_blocks, own_step, 0)

    @when(z == 0)
    def _():
        rpo[0] = jnp.zeros(rpo.shape[1:], bf16)
        rpd[0] = jnp.zeros(rpd.shape[1:], bf16)

    @when(z == Z - 1)
    def _():
        rpo[Z] = jnp.zeros(rpo.shape[1:], bf16)
        rpd[Z] = jnp.zeros(rpd.shape[1:], bf16)

    pq_copy = remote(psend, pown.at[pl.ds(cap, cap), :], pq_s.at[0], pq_r.at[0], ee=partner)
    pq_copy.start()

    def zo_copy(q, d, slot, to):
        rows = pl.ds((q - 2) * cap, cap)
        return remote(po.at[d, rows, :], rpo.at[slot, rows, :], zo_s.at[q, d], zo_r.at[q, slot], zz=to)

    def back_slot(d, to):
        return Z if d == to else d

    def zo_edge(q, i):
        @when(z == 0)
        def _():
            zo_copy(q, Z - 1 - i, Z - 1 - i, 1).start()

        @when(z == Z - 1)
        def _():
            zo_copy(q, i, back_slot(i, Z - 2), Z - 2).start()

    def expert_unit(q):
        for t in range(2, Z - 1):
            gather(q, t)
        for at, s in ends:
            @when(z == at)
            def _():
                dx_copy(q, 1, s).wait_recv()
        hidden(lambda: arrived[q * cap:(q + 1) * cap, :], cap, ein)
        rows = slice((q - 2) * cap, (q - 1) * cap)
        for i in range(Z):
            d = (1 - upper) * (Z - 1 - i) + upper * i

            def step(k, carry):
                acc = jnp.dot(hbuf[0:cap, :], eout[:, pl.ds(pl.multiple_of(d * share + k * 256, 256), 256)],
                              preferred_element_type=f32)
                po[d, rows, pl.ds(pl.multiple_of(k * 256, 256), 256)] = acc.astype(bf16)
                return carry

            lax.fori_loop(0, share // 256, step, 0)
            if i > 0:
                zo_edge(q, i - 1)

    def zo_up(q, d):
        @when((z > 0) & (z < d))
        def _():
            rows = slice((q - 2) * cap, (q - 1) * cap)
            zo_copy(q, d, d, above).wait_recv()
            po[d, rows, :] = (po[d, rows, :].astype(f32) + rpo[d, rows, :].astype(f32)).astype(bf16)
            zo_copy(q, d, d, above).start()

    def zo_down(q, d):
        @when((z < Z - 1) & (z > d))
        def _():
            rows = slice((q - 2) * cap, (q - 1) * cap)
            zo_copy(q, d, d, below).wait_recv()
            po[d, rows, :] = (po[d, rows, :].astype(f32) + rpo[d, rows, :].astype(f32)).astype(bf16)

        for slot, near in ((d, z > d + 1), (Z, z == d + 1)):
            @when((z < Z - 1) & near)
            def _():
                zo_copy(q, d, slot, below).start()

    def zo_pass(q, t):
        @when(upper == 0)
        def _():
            zo_up(q, Z - 1 - t)
            zo_down(q, t)

        @when(upper == 1)
        def _():
            zo_down(q, t)
            zo_up(q, Z - 1 - t)

    def ret_copy(q):
        rows = pl.ds((q - 2) * cap, cap)
        return remote(ret.at[rows, :], rret.at[rows, :], ret_s.at[q], ret_r.at[q], ee=expert_at(-(q // 2), q % 2))

    def zo_final(q):
        @when(z > 0)
        def _():
            zo_copy(q, z, z, above).wait_recv()

        @when(z < Z - 1)
        def _():
            zo_copy(q, z, Z, above).wait_recv()
        rows = slice((q - 2) * cap, (q - 1) * cap)
        ret[rows, :] = (po[z, rows, :].astype(f32) + rpo[z, rows, :].astype(f32)
                        + rpo[Z, rows, :].astype(f32)).astype(bf16)

    for q in units:
        expert_unit(q)
        take(EARLY + 1)

    first = SUBS[0]
    half = [q for q in units][:max(1, len(units) // 2)] if len(units) else []
    rest = [q for q in units][len(half):]
    for t in range(Z - 1):
        for q in half:
            zo_pass(q, t)
        take(EARLY + 2 + t)
        relay(EARLY + 1 + t)
    for q in half:
        zo_final(q)
    take(first)
    relay(first)
    locals_[3].wait()
    own_copies[0].wait_recv()
    collect(0, range(SUBS[0]))
    for q in half:
        ret_copy(q).start()
    for i in range(4):
        hidden(lambda: normed[...], T, win, *part_of(i, 4))
        if i < Z - 1:
            for q in rest:
                zo_pass(q, i)
        if i in (0, 2):
            take(first + 1 + i // 2)
    for t in range(4, Z - 1):
        for q in rest:
            zo_pass(q, t)

    def zd_copy(d, slot, c, to):
        cols = pl.ds(c * wide, wide)
        return remote(pd.at[d, :, cols], rpd.at[slot, :, cols], zd_s.at[d, c], zd_r.at[slot, c], zz=to)

    locals_[4].wait()
    own_copies[1].wait_recv()
    pq_copy.wait_recv()
    mine = Z // C if Z % C == 0 else 0

    def slice_number(i):
        if C == 2 and Z % 2 == 0:
            low = i if i < mine else Z - 1 - (i - mine)
            return chip * (Z - 1 - low) + (1 - chip) * low
        return lax.rem(chip * mine + i, Z)

    def dense(i, c):
        d = slice_number(i)

        def step(k, carry):
            cols = pl.ds(pl.multiple_of(d * share + c * wide + k * tn, tn), tn)
            acc = jnp.dot(hbuf[0:T, :], wout[:, cols], preferred_element_type=f32)
            res = jnp.dot(pk[...], pown[:, cols], preferred_element_type=f32)
            pd[d, :, pl.ds(pl.multiple_of(c * wide + k * tn, tn), tn)] = (acc + gate[...] * res).astype(bf16)
            return carry

        lax.fori_loop(0, wide // tn, step, 0)

        @when((z == 0) & (d > 0))
        def _():
            zd_copy(d, d, c, above).start()

        for slot, near in ((d, z > d + 1), (Z, z == d + 1)):
            @when((z == Z - 1) & near)
            def _():
                zd_copy(d, slot, c, below).start()

    def zd_pass(i, c):
        d = slice_number(i)
        cols = pl.ds(c * wide, wide)

        @when((z > 0) & (z < Z - 1) & (z != d))
        def _():
            zd_copy(d, d, c, above).wait_recv()
            pd[d, :, cols] = (pd[d, :, cols].astype(f32) + rpd[d, :, cols].astype(f32)).astype(bf16)

        @when((z > 0) & (z < d))
        def _():
            zd_copy(d, d, c, above).start()

        for slot, near in ((d, z > d + 1), (Z, z == d + 1)):
            @when((z < Z - 1) & near)
            def _():
                zd_copy(d, slot, c, below).start()

    trow = min(128, T)
    residual = slice_at(z)

    def combine_experts():
        for q in units:
            ret_copy(q).wait_recv()
        for i in range(T // trow):
            rows = slice(i * trow, (i + 1) * trow)
            res = jnp.zeros((trow, share), f32)
            for q in units:
                wanted = slot_col[rows, :] - (expert_at(q // 2, q % 2) * cap).astype(f32)
                pick = (lax.broadcasted_iota(jnp.int32, (trow, cap), 1).astype(f32) == wanted)
                res = res + jnp.dot(pick.astype(f32).astype(bf16), rret[(q - 2) * cap:(q - 1) * cap, :],
                                    preferred_element_type=f32)
            base[rows, :] = tok[rows, residual].astype(f32) + gate[rows, :] * res

    def finish(c):
        cols = slice(c * wide, (c + 1) * wide)

        @when(z > 0)
        def _():
            zd_copy(z, z, c, above).wait_recv()

        @when(z < Z - 1)
        def _():
            zd_copy(z, Z, c, above).wait_recv()

        for i in range(T // trow):
            rows = slice(i * trow, (i + 1) * trow)
            total = pd[z, rows, cols].astype(f32) + rpd[z, rows, cols].astype(f32) + rpd[Z, rows, cols].astype(f32)
            out[rows, cols] = (base[rows, cols] + total).astype(bf16)

    per = SUBS[1] // nk
    for i in range(mine):
        for c in range(nk):
            dense(i, c)
    for q in rest:
        zo_final(q)
    for c in range(nk):
        last = first + (c + 1) * per
        take(last)
        if c == 0:
            for q in rest:
                ret_copy(q).start()
        relay(last)
        collect(1, range(c * per, (c + 1) * per))
        for i in range(mine, Z):
            dense(i, c)
        if c == 0:
            for i in range(mine):
                for k in range(nk):
                    zd_pass(i, k)
    combine_experts()
    for c in range(nk):
        for i in range(mine, Z):
            zd_pass(i, c)
        finish(c)

    for copy in own_copies:
        copy.wait_send()
    d1_copy.wait_send()
    pq_copy.wait_send()
    for q in units:
        dx_copy(q, 0, z).wait_send()
        ret_copy(q).wait_send()
        for at, s in ends:
            @when(z == at)
            def _():
                dx_copy(q, 1, s).wait_send()
        for t in range(1, Z - 1):
            @when((z >= t - 1) & (z < Z - 1))
            def _():
                hop(q, 0, t, z - t + 1).wait_send()

            @when((z + t - 1 <= Z - 1) & (z > 0))
            def _():
                hop(q, 1, t, z + t - 1).wait_send()
    for m in range(2):
        for s in range(SUBS[m]):
            for kc in range(1, C):
                x_copy(m, kc, s).wait_send()
                for dg in range(1, G):
                    y_copy(m, kc, s, dg).wait_send()
                for dg in range(G):
                    p_copy(m, kc, s, dg).wait_send()
    for d in range(Z):
        @when(z != d)
        def _():
            for q in units:
                zo_copy(q, d, d, above).wait_send()
            for c in range(nk):
                zd_copy(d, d, c, above).wait_send()


def local(tokens, route, gate_prob, norm_gain, dense_in, dense_out, expert_in, expert_out):
    G, E, Z = lax.axis_size("groups"), lax.axis_size("expert"), lax.axis_size("cuts")
    T, D = tokens.shape
    F = dense_in.shape[1]
    share = D // Z
    De = D // E
    cap = max(2, 3 * T // (2 * E))
    C = E // 2
    others = (E - 2) * cap
    nk = 2 if De == share and share % 256 == 0 else 1
    bf16 = jnp.bfloat16
    any_, vmem = pl.BlockSpec(memory_space=pl.ANY), pl.BlockSpec(memory_space=pltpu.VMEM)
    dma = pltpu.SemaphoreType.DMA
    subs = max(SUBS)
    return pl.pallas_call(
        functools.partial(kernel, G, E, Z, cap, nk),
        out_shape=jax.ShapeDtypeStruct((T, share), bf16),
        in_specs=[any_, vmem, vmem, vmem, any_, any_, any_, any_],
        out_specs=vmem,
        scratch_shapes=[
            pltpu.VMEM((D, F), bf16), pltpu.VMEM((F, D), bf16),
            pltpu.VMEM((D, F), bf16), pltpu.VMEM((F, D), bf16),
            pltpu.VMEM((T, D), bf16), pltpu.VMEM((T, D), bf16),
            pltpu.VMEM((2, others, share), bf16), pltpu.VMEM((cap, D), bf16), pltpu.VMEM((E * cap, D), bf16),
            pltpu.VMEM((max(T, 2 * cap), F), bf16),
            pltpu.VMEM((2 * cap, D), bf16), pltpu.VMEM((cap, D), bf16),
            pltpu.VMEM((Z, others, share), bf16), pltpu.VMEM((Z + 1, others, share), bf16),
            pltpu.VMEM((Z, T, share), bf16), pltpu.VMEM((Z + 1, T, share), bf16),
            pltpu.VMEM((others, share), bf16), pltpu.VMEM((others, share), bf16),
            pltpu.VMEM((T, share), jnp.float32), pltpu.VMEM((T, 2 * cap), bf16),
            dma((5,)), dma((2,)), dma((2,)), dma((1,)), dma((1,)), dma((E, 2)), dma((E, 2)),
            dma((E, 2, Z)), dma((E, 2, Z)), dma((1,)), dma((1,)),
            dma((2, C, subs)), dma((2, C, subs)),
            dma((2, C, subs, G)), dma((2, C, subs, G)), dma((2, C, subs, G)), dma((2, C, subs, G)),
            dma((E, Z)), dma((E, Z + 1)), dma((Z, nk)), dma((Z + 1, nk)), dma((E,)), dma((E,)),
        ],
        compiler_params=pltpu.CompilerParams(
            collective_id=0, has_side_effects=True, vmem_limit_bytes=67043328
        ),
    )(tokens, route, gate_prob[:, None], norm_gain[None, :], dense_in, dense_out, expert_in, expert_out)


def solution(mesh):
    return jax.shard_map(
        local,
        mesh=mesh,
        in_specs=(
            P(("groups", "expert"), None),
            P(("groups", "expert"), None),
            P(("groups", "expert")),
            P(),
            P("expert", "cuts"),
            P("cuts", "expert"),
            P("expert", None, "cuts"),
            P("expert", "cuts", None),
        ),
        out_specs=P(("groups", "expert"), "cuts"),
        check_vma=False,
    )
```

time: 144 us -> 151 us (1.049); the launches traced: 141 us -> 151 us
  Pallas kernels: 136 us -> 146 us
    pallas_call x1, Pallas kernels: 136 us -> 146 us  [local(): pl.pallas_call(functools.partial(kernel, G, E, Z, cap, nk), out_shape=jax...]
where the time goes in v1:
time: 151 us
  Pallas kernels  146 us (97%)
  local copies, waits for them, and re-layouts  4.94 us (3%)
    pallas_call x1, Pallas kernels, local(): pl.pallas_call(functools.partial(kernel, G, E, Z, cap, nk), out_shape=jax...  146 us
    unnamed x2, local copies, waits for them, and re-layouts  3.4 us

profile of v1, /device:TPU:2, one launch (start us, length us, event | category | flops | bytes accessed | tf_op | source)
XLA Modules:
  0.0 151.2 jit_solution(2273329337109423143)
XLA Ops:
  0.0 1.5 %copy.10.route = s32[512,1]{1,0:T(8,128)} copy(s32[512,1]{0,1:T(1,128)} %param.9) | data formatting | bytes 4096 | tf_op args[1]
  1.5 1.5 %copy.11.gate = f32[512,1]{1,0:T(8,128)} copy(f32[512,1]{0,1:T(1,128)} %bitcast.3) | data formatting | bytes 4096 | tf_op jit(solution)/shard_map/broadcast_in_dim | solution.py:614
  3.1 146.3 %shard_map.82 = bf16[512,512]{1,0:T(8,128)(2,1)} custom-call(bf16[512,2048]{1,0:T(8,128)(2,1)} %tokens.1, s32[512,1]{1,0:T(8,128)} %copy.10.route, f32[512,1]{1,0:T(8,128)} %copy.11.gate, f32[1,2048]{1,0:T(1,128)} %bitcast.2, bf16[512,2048]{1,0:T(8,128)(2,1)} %din.1, bf16[2048,512]{1,0:T(8,128)(2,1)} %dout.1, bf16[1,2048,2048]{2,1,0:T(8,128)(2,1)} %ein_h.1, ...), custom_call_target="tpu_custom_call" | custom-call | tf_op jit(solution)/shard_map/pallas_call | solution.py:589
  149.4 1.9 %copy.13 = bf16[512,512]{1,0:T(8,128)(2,1)} copy(bf16[512,512]{1,0:T(8,128)(2,1)} %shard_map.82) | data formatting | bytes 1048576

commit v2 on v1

--- a/solution.py
+++ b/solution.py
@@ -7,13 +7,12 @@
 from jax.experimental.pallas import tpu as pltpu
 from jax.sharding import PartitionSpec as P
 
-SUBS = (4, 4)
 EARLY = 1
 
 
-def kernel(G, E, Z, cap, nk, tokens, route, gate, gain, din, dout, ein_h, eout_h, out,
+def kernel(G, E, Z, cap, nk, SUBS, tokens, route, gate, gain, din, dout, ein_h, eout_h, out,
            win, wout, ein, eout, tok, normed, disp, dispq, arrived, hbuf, pown, psend, po, rpo, pd, rpd,
-           ret, rret, base, pk,
+           ret, rret, base, pk, turned,
            loc, own_s, own_r, d1_s, d1_r, dx_s, dx_r, ag_s, ag_r, pq_s, pq_r,
            wx_s, wx_r, wy_s, wy_r, wp_s, wp_r, zo_s, zo_r, zd_s, zd_r, ret_s, ret_r):
     f32, bf16 = jnp.float32, jnp.bfloat16
@@ -25,6 +24,7 @@
     wide = share // nk
     tn = min(256, wide)
     units = range(2, E)
+    fast, slow = units[:(E - 2) // 2], units[(E - 2) // 2:]
     g, e, z = lax.axis_index("groups"), lax.axis_index("expert"), lax.axis_index("cuts")
     chip, core = e // 2, lax.rem(e, 2)
     partner = chip * 2 + 1 - core
@@ -159,12 +159,12 @@
     lax.fori_loop(0, T // nrow, norm_step, 0)
 
     picked = route[...]
-    one_hot = (lax.broadcasted_iota(jnp.int32, (T, 128), 1) == picked).astype(f32)
-    lower = (lax.broadcasted_iota(jnp.int32, (T, T), 1) < lax.broadcasted_iota(jnp.int32, (T, T), 0))
-    before = jnp.dot(lower.astype(f32).astype(bf16), one_hot.astype(bf16), preferred_element_type=f32)
-    position = jnp.sum(before * one_hot, axis=1, keepdims=True)
-    slot_col = picked.astype(f32) * float(cap) + position
-    slot_row = jnp.transpose(jnp.broadcast_to(slot_col, (T, 128)))[0:1, :]
+    lanes = -(-E // 8) * 8
+    one_hot = (lax.broadcasted_iota(jnp.int32, (lanes, T), 0) == picked).astype(f32)
+    earlier = (lax.broadcasted_iota(jnp.int32, (T, T), 0) < lax.broadcasted_iota(jnp.int32, (T, T), 1))
+    before = jnp.dot(one_hot.astype(bf16), earlier.astype(f32).astype(bf16), preferred_element_type=f32)
+    position = jnp.sum(before * one_hot, axis=0, keepdims=True)
+    slot_row = picked.astype(f32) * float(cap) + position
 
     def slice_at(s):
         return pl.ds(pl.multiple_of(s * share, share), share)
@@ -206,7 +206,7 @@
     for at, s in ends:
         @when(z == at)
         def _():
-            for q in units:
+            for q in fast:
                 fill_slice(q, 1, s)
     if pending is not None:
         dx_copy(pending, 0, z).start()
@@ -214,7 +214,7 @@
     for at, s in ends:
         @when(z == at)
         def _():
-            for q in units:
+            for q in fast:
                 dx_copy(q, 1, s).start()
     issue(len(steps))
     fill(0, arrived)
@@ -226,6 +226,9 @@
         part = arrived.at[pl.ds(q * cap, cap), slice_at(s)]
         return remote(part, part, ag_s.at[q, way, t], ag_r.at[q, way, t], zz=below if way else above)
 
+    def hops(q):
+        return Z - 2 if q in fast else Z - 1
+
     def gather(q, t):
         if t == 0:
             dx_copy(q, 0, z).wait_recv()
@@ -234,7 +237,7 @@
         def _():
             if t > 0:
                 hop(q, 0, t, z - t).wait_recv()
-        if t < Z - 2:
+        if t < hops(q):
             @when((z >= t) & (z < Z - 1))
             def _():
                 hop(q, 0, t + 1, z - t).start()
@@ -243,7 +246,7 @@
         def _():
             if t > 0:
                 hop(q, 1, t, z + t).wait_recv()
-        if t < Z - 2:
+        if t < hops(q):
             @when((z + t <= Z - 1) & (z > 0))
             def _():
                 hop(q, 1, t + 1, z + t).start()
@@ -264,6 +267,9 @@
 
     pair = 2 * cap
     take(EARLY)
+    first_row = lax.broadcasted_iota(jnp.int32, (128, T), 0) == 0
+    turned[...] = jnp.transpose(jnp.where(first_row, slot_row, gate[...]))
+    slot_col = turned[:, 0:1]
     col = lax.broadcasted_iota(jnp.int32, (T, pair), 1).astype(f32)
     here = slot_col - (e * cap).astype(f32)
     there = slot_col - (partner * cap).astype(f32) + float(cap)
@@ -323,14 +329,15 @@
         def _():
             zo_copy(q, i, back_slot(i, Z - 2), Z - 2).start()
 
-    def expert_unit(q):
-        for t in range(2, Z - 1):
-            gather(q, t)
-        for at, s in ends:
-            @when(z == at)
-            def _():
-                dx_copy(q, 1, s).wait_recv()
+    def expert_hidden(q):
+        if q in fast:
+            for at, s in ends:
+                @when(z == at)
+                def _():
+                    dx_copy(q, 1, s).wait_recv()
         hidden(lambda: arrived[q * cap:(q + 1) * cap, :], cap, ein)
+
+    def expert_out(q, between=None):
         rows = slice((q - 2) * cap, (q - 1) * cap)
         for i in range(Z):
             d = (1 - upper) * (Z - 1 - i) + upper * i
@@ -344,6 +351,8 @@
             lax.fori_loop(0, share // 256, step, 0)
             if i > 0:
                 zo_edge(q, i - 1)
+            if between is not None and i == Z // 2 - 1:
+                between()
 
     def zo_up(q, d):
         @when((z > 0) & (z < d))
@@ -365,15 +374,22 @@
             def _():
                 zo_copy(q, d, slot, below).start()
 
-    def zo_pass(q, t):
+    def zo_near(q, t):
         @when(upper == 0)
         def _():
             zo_up(q, Z - 1 - t)
+
+        @when(upper == 1)
+        def _():
             zo_down(q, t)
 
+    def zo_far(q, t):
+        @when(upper == 0)
+        def _():
+            zo_down(q, t)
+
         @when(upper == 1)
         def _():
-            zo_down(q, t)
             zo_up(q, Z - 1 - t)
 
     def ret_copy(q):
@@ -392,37 +408,62 @@
         ret[rows, :] = (po[z, rows, :].astype(f32) + rpo[z, rows, :].astype(f32)
                         + rpo[Z, rows, :].astype(f32)).astype(bf16)
 
-    for q in units:
-        expert_unit(q)
-        take(EARLY + 1)
-
-    first = SUBS[0]
-    half = [q for q in units][:max(1, len(units) // 2)] if len(units) else []
-    rest = [q for q in units][len(half):]
-    for t in range(Z - 1):
-        for q in half:
-            zo_pass(q, t)
-        take(EARLY + 2 + t)
-        relay(EARLY + 1 + t)
-    for q in half:
-        zo_final(q)
-    take(first)
-    relay(first)
+    def point(n):
+        return n * SUBS[0] // 8 if n <= 8 else SUBS[0] + (n - 8) * SUBS[1] // 8
+
+    def weights(to_take, to_relay):
+        take(point(to_take))
+        relay(point(to_relay))
+
+    def passes(kind, group, t):
+        if t < Z - 1:
+            for q in group:
+                kind(q, t)
+
+    for t in range(2, Z - 1):
+        for q in fast:
+            gather(q, t)
+    take(point(2))
+    for n, q in enumerate(fast):
+        expert_hidden(q)
+        if n == len(fast) - 1:
+            for k in slow:
+                for t in range(2, Z - 1):
+                    gather(k, t)
+        expert_out(q)
+    weights(4, 2)
+    for n, q in enumerate(slow):
+        gather(q, Z - 1)
+        if n == 0:
+            take(point(5))
+        expert_hidden(q)
+        if n == len(slow) - 1:
+            weights(6, 3)
+        expert_out(q, (lambda: weights(7, 5)) if n == len(slow) - 1 else None)
+    weights(8, 6)
+    passes(zo_near, fast, 0)
+    passes(zo_far, fast, 0)
+    passes(zo_near, fast, 1)
+    weights(9, 8)
+    passes(zo_far, fast, 1)
+    for t in range(2, Z - 1):
+        passes(zo_near, fast, t)
+        passes(zo_far, fast, t)
     locals_[3].wait()
     own_copies[0].wait_recv()
     collect(0, range(SUBS[0]))
-    for q in half:
-        ret_copy(q).start()
-    for i in range(4):
+
+    def mlp_hidden(i):
         hidden(lambda: normed[...], T, win, *part_of(i, 4))
-        if i < Z - 1:
-            for q in rest:
-                zo_pass(q, i)
-        if i in (0, 2):
-            take(first + 1 + i // 2)
-    for t in range(4, Z - 1):
-        for q in rest:
-            zo_pass(q, t)
+
+    mlp_hidden(0)
+    weights(10, 8)
+    mlp_hidden(1)
+    weights(11, 9)
+    mlp_hidden(2)
+    passes(zo_near, slow, 0)
+    mlp_hidden(3)
+    weights(12, 10)
 
     def zd_copy(d, slot, c, to):
         cols = pl.ds(c * wide, wide)
@@ -439,6 +480,9 @@
             return chip * (Z - 1 - low) + (1 - chip) * low
         return lax.rem(chip * mine + i, Z)
 
+    def late(i, c):
+        return c == nk - 1 and nk > 1 and i == 1 and mine > 1
+
     def dense(i, c):
         d = slice_number(i)
 
@@ -446,17 +490,26 @@
             cols = pl.ds(pl.multiple_of(d * share + c * wide + k * tn, tn), tn)
             acc = jnp.dot(hbuf[0:T, :], wout[:, cols], preferred_element_type=f32)
             res = jnp.dot(pk[...], pown[:, cols], preferred_element_type=f32)
-            pd[d, :, pl.ds(pl.multiple_of(c * wide + k * tn, tn), tn)] = (acc + gate[...] * res).astype(bf16)
+            pd[d, :, pl.ds(pl.multiple_of(c * wide + k * tn, tn), tn)] = (acc + turned[:, 1:2] * res).astype(bf16)
             return carry
 
         lax.fori_loop(0, wide // tn, step, 0)
 
-        @when((z == 0) & (d > 0))
+        dense_edge(i, c, False)
+
+    def dense_edge(i, c, again):
+        d = slice_number(i)
+        beside = ((z == 0) & (d == 1)) | ((z == Z - 1) & (d == Z - 2))
+        go = (beside if again else ~beside) if late(i, c) else True
+        if again and not late(i, c):
+            return
+
+        @when((z == 0) & (d > 0) & go)
         def _():
             zd_copy(d, d, c, above).start()
 
         for slot, near in ((d, z > d + 1), (Z, z == d + 1)):
-            @when((z == Z - 1) & near)
+            @when((z == Z - 1) & near & go)
             def _():
                 zd_copy(d, slot, c, below).start()
 
@@ -488,11 +541,40 @@
             rows = slice(i * trow, (i + 1) * trow)
             res = jnp.zeros((trow, share), f32)
             for q in units:
-                wanted = slot_col[rows, :] - (expert_at(q // 2, q % 2) * cap).astype(f32)
+                wanted = turned[rows, 0:1] - (expert_at(q // 2, q % 2) * cap).astype(f32)
                 pick = (lax.broadcasted_iota(jnp.int32, (trow, cap), 1).astype(f32) == wanted)
                 res = res + jnp.dot(pick.astype(f32).astype(bf16), rret[(q - 2) * cap:(q - 1) * cap, :],
                                     preferred_element_type=f32)
-            base[rows, :] = tok[rows, residual].astype(f32) + gate[rows, :] * res
+            base[rows, :] = tok[rows, residual].astype(f32) + turned[rows, 1:2] * res
+
+    def sent():
+        for copy in own_copies:
+            copy.wait_send()
+        d1_copy.wait_send()
+        pq_copy.wait_send()
+        for q in units:
+            dx_copy(q, 0, z).wait_send()
+            ret_copy(q).wait_send()
+            for at, s in ends:
+                @when((z == at) & (q in fast))
+                def _():
+                    dx_copy(q, 1, s).wait_send()
+            for t in range(1, hops(q) + 1):
+                @when((z >= t - 1) & (z < Z - 1))
+                def _():
+                    hop(q, 0, t, z - t + 1).wait_send()
+
+                @when((z + t - 1 <= Z - 1) & (z > 0))
+                def _():
+                    hop(q, 1, t, z + t - 1).wait_send()
+        for m in range(2):
+            for s in range(SUBS[m]):
+                for kc in range(1, C):
+                    x_copy(m, kc, s).wait_send()
+                    for dg in range(1, G):
+                        y_copy(m, kc, s, dg).wait_send()
+                    for dg in range(G):
+                        p_copy(m, kc, s, dg).wait_send()
 
     def finish(c):
         cols = slice(c * wide, (c + 1) * wide)
@@ -511,58 +593,52 @@
             out[rows, cols] = (base[rows, cols] + total).astype(bf16)
 
     per = SUBS[1] // nk
-    for i in range(mine):
-        for c in range(nk):
+    for c in range(nk):
+        for i in range(mine):
             dense(i, c)
-    for q in rest:
-        zo_final(q)
+        if c == 0:
+            weights(13, 11)
+            passes(zo_near, slow, 1)
+            passes(zo_far, slow, 0)
+            passes(zo_far, slow, 1)
+            for t in range(2, Z - 1):
+                passes(zo_near, slow, t)
+                passes(zo_far, slow, t)
+            for q in fast:
+                zo_final(q)
+                ret_copy(q).start()
     for c in range(nk):
-        last = first + (c + 1) * per
-        take(last)
-        if c == 0:
-            for q in rest:
-                ret_copy(q).start()
-        relay(last)
+        if c == nk - 1:
+            weights(15, 13)
+            weights(16, 14)
+            weights(16, 15)
+            weights(16, 16)
+        else:
+            weights(14, 12)
         collect(1, range(c * per, (c + 1) * per))
         for i in range(mine, Z):
             dense(i, c)
         if c == 0:
-            for i in range(mine):
-                for k in range(nk):
-                    zd_pass(i, k)
-    combine_experts()
+            for q in slow:
+                zo_final(q)
+                ret_copy(q).start()
     for c in range(nk):
-        for i in range(mine, Z):
-            zd_pass(i, c)
+        for i in range(Z):
+            dense_edge(i, c, True)
+    low_first = list(range(Z)) if mine == 0 else list(range(mine, Z)) + list(range(mine))
+    turn = lax.rem(upper + chip, 2) if C == 2 else upper
+    for c in range(nk):
+        for flag, order in ((0, low_first), (1, list(range(Z)))):
+            @when(turn == flag)
+            def _():
+                for i in order if C == 2 else range(Z):
+                    zd_pass(i, c)
+        if c == 0:
+            combine_experts()
+            sent()
+    for c in range(nk):
         finish(c)
 
-    for copy in own_copies:
-        copy.wait_send()
-    d1_copy.wait_send()
-    pq_copy.wait_send()
-    for q in units:
-        dx_copy(q, 0, z).wait_send()
-        ret_copy(q).wait_send()
-        for at, s in ends:
-            @when(z == at)
-            def _():
-                dx_copy(q, 1, s).wait_send()
-        for t in range(1, Z - 1):
-            @when((z >= t - 1) & (z < Z - 1))
-            def _():
-                hop(q, 0, t, z - t + 1).wait_send()
-
-            @when((z + t - 1 <= Z - 1) & (z > 0))
-            def _():
-                hop(q, 1, t, z + t - 1).wait_send()
-    for m in range(2):
-        for s in range(SUBS[m]):
-            for kc in range(1, C):
-                x_copy(m, kc, s).wait_send()
-                for dg in range(1, G):
-                    y_copy(m, kc, s, dg).wait_send()
-                for dg in range(G):
-                    p_copy(m, kc, s, dg).wait_send()
     for d in range(Z):
         @when(z != d)
         def _():
@@ -585,9 +661,10 @@
     bf16 = jnp.bfloat16
     any_, vmem = pl.BlockSpec(memory_space=pl.ANY), pl.BlockSpec(memory_space=pltpu.VMEM)
     dma = pltpu.SemaphoreType.DMA
-    subs = max(SUBS)
+    splits = (max(1, min(8, De // (16 * G))), 8)
+    subs = max(splits)
     return pl.pallas_call(
-        functools.partial(kernel, G, E, Z, cap, nk),
+        functools.partial(kernel, G, E, Z, cap, nk, splits),
         out_shape=jax.ShapeDtypeStruct((T, share), bf16),
         in_specs=[any_, vmem, vmem, vmem, any_, any_, any_, any_],
         out_specs=vmem,
@@ -602,6 +679,7 @@
             pltpu.VMEM((Z, T, share), bf16), pltpu.VMEM((Z + 1, T, share), bf16),
             pltpu.VMEM((others, share), bf16), pltpu.VMEM((others, share), bf16),
             pltpu.VMEM((T, share), jnp.float32), pltpu.VMEM((T, 2 * cap), bf16),
+            pltpu.VMEM((T, 128), jnp.float32),
             dma((5,)), dma((2,)), dma((2,)), dma((1,)), dma((1,)), dma((E, 2)), dma((E, 2)),
             dma((E, 2, Z)), dma((E, 2, Z)), dma((1,)), dma((1,)),
             dma((2, C, subs)), dma((2, C, subs)),
@@ -611,7 +689,7 @@
         compiler_params=pltpu.CompilerParams(
             collective_id=0, has_side_effects=True, vmem_limit_bytes=67043328
         ),
-    )(tokens, route, gate_prob[:, None], norm_gain[None, :], dense_in, dense_out, expert_in, expert_out)
+    )(tokens, route.reshape(1, T), gate_prob[None, :], norm_gain[None, :], dense_in, dense_out, expert_in, expert_out)
 
 
 def solution(mesh):

time: 151 us -> 120 us (0.79)
  Pallas kernels: 146 us -> 118 us
  local copies, waits for them, and re-layouts: 4.94 us -> 1.87 us
    pallas_call x1, Pallas kernels: 146 us -> 118 us  [local(): pl.pallas_call(functools.partial(kernel, G, E, Z, cap, nk, splits), out_s...]
    unnamed x2 -> x1, local copies, waits for them, and re-layouts: 3.4 us -> 1.87 us
    broadcast_in_dim x1 -> x0, local copies, waits for them, and re-layouts: 1.53 us -> none  [local(): gate_prob[:, None]]
where the time goes in v2:
time: 120 us
  Pallas kernels  118 us (98%)
  local copies, waits for them, and re-layouts  1.87 us (2%)
    pallas_call x1, Pallas kernels, local(): pl.pallas_call(functools.partial(kernel, G, E, Z, cap, nk, splits), out_s...  118 us

profile of v2, /device:TPU:2, one launch (start us, length us, event | category | flops | bytes accessed | tf_op | source)
XLA Modules:
  0.0 120.0 jit_solution(17240337741604765540)
XLA Ops:
  0.0 118.1 %shard_map.82 = bf16[512,512]{1,0:T(8,128)(2,1)} custom-call(bf16[512,2048]{1,0:T(8,128)(2,1)} %tokens.1, s32[1,512]{1,0:T(1,128)} %bitcast.4, f32[1,512]{1,0:T(1,128)} %bitcast.5, f32[1,2048]{1,0:T(1,128)} %bitcast.3, bf16[512,2048]{1,0:T(8,128)(2,1)} %din.1, bf16[2048,512]{1,0:T(8,128)(2,1)} %dout.1, bf16[1,2048,2048]{2,1,0:T(8,128)(2,1)} %ein_h.1, ...), custom_call_target="tpu_custom_call" | custom-call | tf_op jit(solution)/shard_map/pallas_call | solution.py:666
  118.2 1.9 %copy.10 = bf16[512,512]{1,0:T(8,128)(2,1)} copy(bf16[512,512]{1,0:T(8,128)(2,1)} %shard_map.82) | data formatting | bytes 1048576

commit v3 on v2

--- a/solution.py
+++ b/solution.py
@@ -12,7 +12,7 @@
 
 def kernel(G, E, Z, cap, nk, SUBS, tokens, route, gate, gain, din, dout, ein_h, eout_h, out,
            win, wout, ein, eout, tok, normed, disp, dispq, arrived, hbuf, pown, psend, po, rpo, pd, rpd,
-           ret, rret, base, pk, turned,
+           ret, rret, base, pk, turned, eres,
            loc, own_s, own_r, d1_s, d1_r, dx_s, dx_r, ag_s, ag_r, pq_s, pq_r,
            wx_s, wx_r, wy_s, wy_r, wp_s, wp_r, zo_s, zo_r, zd_s, zd_r, ret_s, ret_r):
     f32, bf16 = jnp.float32, jnp.bfloat16
@@ -96,16 +96,16 @@
         return (din, dout)[m].at[pl.ds(pl.multiple_of(row, n), n), pl.ds(col, width)]
 
     def x_copy(m, kc, s):
-        return remote(weight_source(m, g, s), weight(m, e, g, s), wx_s.at[m, kc, s], wx_r.at[m, kc, s],
+        return remote(weight_source(m, g, s), weight(m, e, g, s), wx_s.at[m], wx_r.at[m, kc - 1, s],
                       ee=expert_at(kc, 0))
 
     def y_copy(m, kc, s, dg):
         w = weight(m, expert_at(-kc, 0), g, s)
-        return remote(w, w, wy_s.at[m, kc, s, dg], wy_r.at[m, kc, s, dg], gg=lax.rem(g + dg, G))
+        return remote(w, w, wy_s.at[m], wy_r.at[m, kc - 1, s, dg - 1], gg=lax.rem(g + dg, G))
 
     def p_copy(m, kc, s, dg):
         w = weight(m, expert_at(-kc, 0), lax.rem(g - dg + G, G), s)
-        return remote(w, w, wp_s.at[m, kc, s, dg], wp_r.at[m, kc, s, dg], ee=partner)
+        return remote(w, w, wp_s.at[m], wp_r.at[m * (1 + s // (SUBS[1] // nk))], ee=partner)
 
     steps = [(m, s) for m in range(2) for s in range(SUBS[m])]
     issued, taken, relayed = [0], [0], [0]
@@ -136,11 +136,12 @@
                 p_copy(m, kc, s, 0).start()
             taken[0] += 1
 
-    def collect(m, subs):
-        for s in subs:
-            for kc in range(1, C):
-                for dg in range(G):
-                    p_copy(m, kc, s, dg).wait_recv()
+    def weight_part(m, rows, cols):
+        return (win, wout)[m].at[pl.ds(0, rows), pl.ds(0, cols)]
+
+    def collect(n):
+        w = weight_part(1, F, (C - 1) * De // nk) if n else weight_part(0, (C - 1) * De, F)
+        remote(w, w, wp_s.at[0], wp_r.at[n], ee=partner).wait_recv()
 
     issue(EARLY)
     locals_[0].wait()
@@ -193,7 +194,7 @@
 
     def dx_copy(q, x, s):
         return remote(disp.at[x, pl.ds((q - 2) * cap, cap), :], arrived.at[pl.ds(q * cap, cap), slice_at(s)],
-                      dx_s.at[q, x], dx_r.at[q, x], ee=expert_at(q // 2, q % 2))
+                      dx_s.at[q - 2, x], dx_r.at[q - 2, x], ee=expert_at(q // 2, q % 2))
 
     d1_copy = remote(dispq, arrived.at[pl.ds(cap, cap), :], d1_s.at[0], d1_r.at[0], ee=partner)
 
@@ -224,7 +225,7 @@
 
     def hop(q, way, t, s):
         part = arrived.at[pl.ds(q * cap, cap), slice_at(s)]
-        return remote(part, part, ag_s.at[q, way, t], ag_r.at[q, way, t], zz=below if way else above)
+        return remote(part, part, ag_s.at[q - 2, way, t - 1], ag_r.at[q - 2, way, t - 1], zz=below if way else above)
 
     def hops(q):
         return Z - 2 if q in fast else Z - 1
@@ -315,7 +316,7 @@
 
     def zo_copy(q, d, slot, to):
         rows = pl.ds((q - 2) * cap, cap)
-        return remote(po.at[d, rows, :], rpo.at[slot, rows, :], zo_s.at[q, d], zo_r.at[q, slot], zz=to)
+        return remote(po.at[d, rows, :], rpo.at[slot, rows, :], zo_s.at[0], zo_r.at[q - 2, slot], zz=to)
 
     def back_slot(d, to):
         return Z if d == to else d
@@ -329,13 +330,17 @@
         def _():
             zo_copy(q, i, back_slot(i, Z - 2), Z - 2).start()
 
-    def expert_hidden(q):
+    def expert_hidden(q, between=None):
         if q in fast:
             for at, s in ends:
                 @when(z == at)
                 def _():
                     dx_copy(q, 1, s).wait_recv()
-        hidden(lambda: arrived[q * cap:(q + 1) * cap, :], cap, ein)
+        rows = slice(q * cap, (q + 1) * cap)
+        hidden(lambda: arrived[rows, :], cap, ein, *part_of(0, 2))
+        if between is not None:
+            between()
+        hidden(lambda: arrived[rows, :], cap, ein, *part_of(1, 2))
 
     def expert_out(q, between=None):
         rows = slice((q - 2) * cap, (q - 1) * cap)
@@ -351,8 +356,8 @@
             lax.fori_loop(0, share // 256, step, 0)
             if i > 0:
                 zo_edge(q, i - 1)
-            if between is not None and i == Z // 2 - 1:
-                between()
+            if between is not None:
+                between(i)
 
     def zo_up(q, d):
         @when((z > 0) & (z < d))
@@ -394,7 +399,7 @@
 
     def ret_copy(q):
         rows = pl.ds((q - 2) * cap, cap)
-        return remote(ret.at[rows, :], rret.at[rows, :], ret_s.at[q], ret_r.at[q], ee=expert_at(-(q // 2), q % 2))
+        return remote(ret.at[rows, :], rret.at[rows, :], ret_s.at[q - 2], ret_r.at[q - 2], ee=expert_at(-(q // 2), q % 2))
 
     def zo_final(q):
         @when(z > 0)
@@ -425,54 +430,78 @@
             gather(q, t)
     take(point(2))
     for n, q in enumerate(fast):
-        expert_hidden(q)
-        if n == len(fast) - 1:
+        final = n == len(fast) - 1
+        expert_hidden(q, (lambda: take(point(3))) if final else None)
+        if final:
             for k in slow:
                 for t in range(2, Z - 1):
                     gather(k, t)
-        expert_out(q)
-    weights(4, 2)
+        expert_out(q, (lambda i: take(point(4))) if final else None)
+    weights(5, 2)
+    pq_copy.wait_recv()
+
+    def own_rows(i, carry):
+        cols = pl.ds(pl.multiple_of(i * 256, 256), 256)
+        res = jnp.dot(pk[...], pown[:, cols], preferred_element_type=f32)
+        eres[:, cols] = (turned[:, 1:2] * res).astype(bf16)
+        return carry
+
+    lax.fori_loop(0, own_blocks, own_rows, 0)
+
+    def serve(i):
+        if i == Z // 2 - 1:
+            relay(point(5))
+            passes(zo_near, fast, 0)
+        if i == Z // 2:
+            weights(8, 6)
+
     for n, q in enumerate(slow):
+        final = n == len(slow) - 1
         gather(q, Z - 1)
         if n == 0:
-            take(point(5))
-        expert_hidden(q)
-        if n == len(slow) - 1:
             weights(6, 3)
-        expert_out(q, (lambda: weights(7, 5)) if n == len(slow) - 1 else None)
-    weights(8, 6)
-    passes(zo_near, fast, 0)
+        expert_hidden(q, (lambda: weights(7, 4)) if final else None)
+        expert_out(q, serve if final else None)
+    passes(zo_near, fast, 1)
+    weights(9, 7)
     passes(zo_far, fast, 0)
-    passes(zo_near, fast, 1)
-    weights(9, 8)
+    relay(point(8))
+    take(point(10))
+    locals_[3].wait()
+    own_copies[0].wait_recv()
+    collect(0)
+
+    def mlp_hidden(i):
+        hidden(lambda: normed[...], T, win, *part_of(i, 4))
+
+    mlp_hidden(0)
+    weights(11, 9)
+    mlp_hidden(1)
+    take(point(12))
     passes(zo_far, fast, 1)
     for t in range(2, Z - 1):
         passes(zo_near, fast, t)
         passes(zo_far, fast, t)
-    locals_[3].wait()
-    own_copies[0].wait_recv()
-    collect(0, range(SUBS[0]))
-
-    def mlp_hidden(i):
-        hidden(lambda: normed[...], T, win, *part_of(i, 4))
-
-    mlp_hidden(0)
-    weights(10, 8)
-    mlp_hidden(1)
-    weights(11, 9)
     mlp_hidden(2)
+    relay(point(10))
     passes(zo_near, slow, 0)
     mlp_hidden(3)
-    weights(12, 10)
-
-    def zd_copy(d, slot, c, to):
-        cols = pl.ds(c * wide, wide)
-        return remote(pd.at[d, :, cols], rpd.at[slot, :, cols], zd_s.at[d, c], zd_r.at[slot, c], zz=to)
+    weights(13, 11)
+
+    nr = 2 if T % 32 == 0 else 1
+    tall = T // nr
+    halves = range(nr)
+
+    def zd_copy(d, slot, c, r, to):
+        rows, cols = pl.ds(r * tall, tall), pl.ds(c * wide, wide)
+        n = c * nr + r
+        return remote(pd.at[d, rows, cols], rpd.at[slot, rows, cols], zd_s.at[0], zd_r.at[slot, n], zz=to)
 
     locals_[4].wait()
     own_copies[1].wait_recv()
-    pq_copy.wait_recv()
     mine = Z // C if Z % C == 0 else 0
+    lined = C == 2 and nk == 2 and mine > 1
+    turn = lax.rem(upper + chip, 2)
 
     def slice_number(i):
         if C == 2 and Z % 2 == 0:
@@ -481,24 +510,24 @@
         return lax.rem(chip * mine + i, Z)
 
     def late(i, c):
-        return c == nk - 1 and nk > 1 and i == 1 and mine > 1
+        return c == nk - 1 and lined and i < mine
 
     def dense(i, c):
         d = slice_number(i)
+        if lined and i < mine:
+            d = turn * d + (1 - turn) * slice_number(mine - 1 - i)
 
         def step(k, carry):
             cols = pl.ds(pl.multiple_of(d * share + c * wide + k * tn, tn), tn)
             acc = jnp.dot(hbuf[0:T, :], wout[:, cols], preferred_element_type=f32)
-            res = jnp.dot(pk[...], pown[:, cols], preferred_element_type=f32)
-            pd[d, :, pl.ds(pl.multiple_of(c * wide + k * tn, tn), tn)] = (acc + turned[:, 1:2] * res).astype(bf16)
+            pd[d, :, pl.ds(pl.multiple_of(c * wide + k * tn, tn), tn)] = (acc + eres[:, cols].astype(f32)).astype(bf16)
             return carry
 
         lax.fori_loop(0, wide // tn, step, 0)
 
-        dense_edge(i, c, False)
-
-    def dense_edge(i, c, again):
-        d = slice_number(i)
+        dense_edge(i, c, False, d)
+
+    def dense_edge(i, c, again, d):
         beside = ((z == 0) & (d == 1)) | ((z == Z - 1) & (d == Z - 2))
         go = (beside if again else ~beside) if late(i, c) else True
         if again and not late(i, c):
@@ -506,30 +535,34 @@
 
         @when((z == 0) & (d > 0) & go)
         def _():
-            zd_copy(d, d, c, above).start()
+            for r in halves:
+                zd_copy(d, d, c, r, above).start()
 
         for slot, near in ((d, z > d + 1), (Z, z == d + 1)):
             @when((z == Z - 1) & near & go)
             def _():
-                zd_copy(d, slot, c, below).start()
+                for r in halves:
+                    zd_copy(d, slot, c, r, below).start()
 
     def zd_pass(i, c):
         d = slice_number(i)
         cols = pl.ds(c * wide, wide)
-
-        @when((z > 0) & (z < Z - 1) & (z != d))
-        def _():
-            zd_copy(d, d, c, above).wait_recv()
-            pd[d, :, cols] = (pd[d, :, cols].astype(f32) + rpd[d, :, cols].astype(f32)).astype(bf16)
-
-        @when((z > 0) & (z < d))
-        def _():
-            zd_copy(d, d, c, above).start()
-
-        for slot, near in ((d, z > d + 1), (Z, z == d + 1)):
-            @when((z < Z - 1) & near)
+        for r in halves:
+            rows = pl.ds(r * tall, tall)
+
+            @when((z > 0) & (z < Z - 1) & (z != d))
             def _():
-                zd_copy(d, slot, c, below).start()
+                zd_copy(d, d, c, r, above).wait_recv()
+                pd[d, rows, cols] = (pd[d, rows, cols].astype(f32) + rpd[d, rows, cols].astype(f32)).astype(bf16)
+
+            @when((z > 0) & (z < d))
+            def _():
+                zd_copy(d, d, c, r, above).start()
+
+            for slot, near in ((d, z > d + 1), (Z, z == d + 1)):
+                @when((z < Z - 1) & near)
+                def _():
+                    zd_copy(d, slot, c, r, below).start()
 
     trow = min(128, T)
     residual = slice_at(z)
@@ -568,24 +601,22 @@
                 def _():
                     hop(q, 1, t, z + t - 1).wait_send()
         for m in range(2):
-            for s in range(SUBS[m]):
-                for kc in range(1, C):
-                    x_copy(m, kc, s).wait_send()
-                    for dg in range(1, G):
-                        y_copy(m, kc, s, dg).wait_send()
-                    for dg in range(G):
-                        p_copy(m, kc, s, dg).wait_send()
+            for sem, n in ((wx_s, 1), (wy_s, G - 1), (wp_s, G)):
+                rows, cols = ((C - 1) * De // G * n, F) if m == 0 else (F // G * n, (C - 1) * De)
+                w = weight_part(m, rows, cols)
+                remote(w, w, sem.at[m], wp_r.at[0], ee=partner).wait_send()
 
     def finish(c):
         cols = slice(c * wide, (c + 1) * wide)
 
-        @when(z > 0)
-        def _():
-            zd_copy(z, z, c, above).wait_recv()
-
-        @when(z < Z - 1)
-        def _():
-            zd_copy(z, Z, c, above).wait_recv()
+        for r in halves:
+            @when(z > 0)
+            def _():
+                zd_copy(z, z, c, r, above).wait_recv()
+
+            @when(z < Z - 1)
+            def _():
+                zd_copy(z, Z, c, r, above).wait_recv()
 
         for i in range(T // trow):
             rows = slice(i * trow, (i + 1) * trow)
@@ -593,59 +624,77 @@
             out[rows, cols] = (base[rows, cols] + total).astype(bf16)
 
     per = SUBS[1] // nk
-    for c in range(nk):
-        for i in range(mine):
-            dense(i, c)
-        if c == 0:
-            weights(13, 11)
-            passes(zo_near, slow, 1)
-            passes(zo_far, slow, 0)
-            passes(zo_far, slow, 1)
-            for t in range(2, Z - 1):
-                passes(zo_near, slow, t)
-                passes(zo_far, slow, t)
-            for q in fast:
-                zo_final(q)
-                ret_copy(q).start()
-    for c in range(nk):
-        if c == nk - 1:
-            weights(15, 13)
-            weights(16, 14)
-            weights(16, 15)
-            weights(16, 16)
-        else:
-            weights(14, 12)
-        collect(1, range(c * per, (c + 1) * per))
+    def along(kind):
+        for i, c in kind:
+            zd_pass(i, c)
+
+    def in_turn(first_kind, second_kind):
+        @when(turn == 0)
+        def _():
+            along(first_kind)
+
+        @when(turn == 1)
+        def _():
+            along(second_kind)
+
+    near, far = list(range(mine, Z)), list(range(mine))
+
+    for i in range(mine):
+        dense(i, 0)
+    weights(14, 12)
+    passes(zo_near, slow, 1)
+    passes(zo_far, slow, 0)
+    if nk > 1:
+        collect(1)
         for i in range(mine, Z):
-            dense(i, c)
-        if c == 0:
-            for q in slow:
-                zo_final(q)
-                ret_copy(q).start()
+            dense(i, 0)
+        weights(15, 13)
+        passes(zo_far, slow, 1)
+        for q in fast:
+            zo_final(q)
+            ret_copy(q).start()
+        for c in range(1, nk):
+            for i in range(mine):
+                dense(i, c)
+    weights(16, 14)
+    for t in range(1 if nk == 1 else 2, Z - 1):
+        passes(zo_near, slow, t)
+        passes(zo_far, slow, t)
+    for q in slow if nk > 1 else units:
+        zo_final(q)
+        ret_copy(q).start()
+    if lined:
+        in_turn([], [(i, 0) for i in far[:1]])
+    relay(point(15))
+    relay(point(16))
+    collect(nk)
+    for i in range(mine, Z):
+        dense(i, nk - 1)
     for c in range(nk):
         for i in range(Z):
-            dense_edge(i, c, True)
-    low_first = list(range(Z)) if mine == 0 else list(range(mine, Z)) + list(range(mine))
-    turn = lax.rem(upper + chip, 2) if C == 2 else upper
-    for c in range(nk):
-        for flag, order in ((0, low_first), (1, list(range(Z)))):
-            @when(turn == flag)
-            def _():
-                for i in order if C == 2 else range(Z):
-                    zd_pass(i, c)
-        if c == 0:
-            combine_experts()
-            sent()
+            dense_edge(i, c, True, slice_number(i))
+    if lined:
+        in_turn([(near[0], 0)], [(i, 0) for i in far[1:]])
+        combine_experts()
+        in_turn([(i, 0) for i in far + near[1:]] + [(near[0], 1)],
+                [(far[0], 1)] + [(i, 0) for i in near] + [(i, 1) for i in far[1:]])
+        sent()
+        in_turn([(i, 1) for i in far + near[1:]], [(i, 1) for i in near])
+    else:
+        for c in range(nk):
+            along([(i, c) for i in range(Z)])
+            if c == 0:
+                combine_experts()
+                sent()
     for c in range(nk):
         finish(c)
 
-    for d in range(Z):
-        @when(z != d)
-        def _():
-            for q in units:
-                zo_copy(q, d, d, above).wait_send()
-            for c in range(nk):
-                zd_copy(d, d, c, above).wait_send()
+    def last_waits():
+        for array, sem in ((po, zo_s), (pd, zd_s)):
+            part = array.at[pl.ds(0, Z - 1)]
+            remote(part, part, sem.at[0], wp_r.at[0], ee=partner).wait_send()
+
+    last_waits()
 
 
 def local(tokens, route, gate_prob, norm_gain, dense_in, dense_out, expert_in, expert_out):
@@ -656,7 +705,8 @@
     De = D // E
     cap = max(2, 3 * T // (2 * E))
     C = E // 2
-    others = (E - 2) * cap
+    away = E - 2
+    others = away * cap
     nk = 2 if De == share and share % 256 == 0 else 1
     bf16 = jnp.bfloat16
     any_, vmem = pl.BlockSpec(memory_space=pl.ANY), pl.BlockSpec(memory_space=pltpu.VMEM)
@@ -679,12 +729,11 @@
             pltpu.VMEM((Z, T, share), bf16), pltpu.VMEM((Z + 1, T, share), bf16),
             pltpu.VMEM((others, share), bf16), pltpu.VMEM((others, share), bf16),
             pltpu.VMEM((T, share), jnp.float32), pltpu.VMEM((T, 2 * cap), bf16),
-            pltpu.VMEM((T, 128), jnp.float32),
-            dma((5,)), dma((2,)), dma((2,)), dma((1,)), dma((1,)), dma((E, 2)), dma((E, 2)),
-            dma((E, 2, Z)), dma((E, 2, Z)), dma((1,)), dma((1,)),
-            dma((2, C, subs)), dma((2, C, subs)),
-            dma((2, C, subs, G)), dma((2, C, subs, G)), dma((2, C, subs, G)), dma((2, C, subs, G)),
-            dma((E, Z)), dma((E, Z + 1)), dma((Z, nk)), dma((Z + 1, nk)), dma((E,)), dma((E,)),
+            pltpu.VMEM((T, 128), jnp.float32), pltpu.VMEM((T, D), bf16),
+            dma((5,)), dma((2,)), dma((2,)), dma((1,)), dma((1,)), dma((away, 2)), dma((away, 2)),
+            dma((away, 2, Z - 1)), dma((away, 2, Z - 1)), dma((1,)), dma((1,)),
+            dma((2,)), dma((2, C - 1, subs)), dma((2,)), dma((2, C - 1, subs, G - 1)), dma((2,)), dma((1 + nk,)),
+            dma((1,)), dma((away, Z + 1)), dma((1,)), dma((Z + 1, 2 * nk)), dma((away,)), dma((away,)),
         ],
         compiler_params=pltpu.CompilerParams(
             collective_id=0, has_side_effects=True, vmem_limit_bytes=67043328

time: 120 us -> 104 us (0.87)
  Pallas kernels: 118 us -> 102 us
    pallas_call x1, Pallas kernels: 118 us -> 102 us  [local(): pl.pallas_call(functools.partial(kernel, G, E, Z, cap, nk, splits), out_s...]
where the time goes in v3:
time: 104 us; the launch traced here: 103 us
  Pallas kernels  102 us (98%)
  local copies, waits for them, and re-layouts  1.87 us (2%)
    pallas_call x1, Pallas kernels, local(): pl.pallas_call(functools.partial(kernel, G, E, Z, cap, nk, splits), out_s...  102 us

profile of v3, /device:TPU:2, one launch (start us, length us, event | category | flops | bytes accessed | tf_op | source)
XLA Modules:
  0.0 103.5 jit_solution(8605973595012696245)
XLA Ops:
  0.0 101.6 %shard_map.82 = bf16[512,512]{1,0:T(8,128)(2,1)} custom-call(bf16[512,2048]{1,0:T(8,128)(2,1)} %tokens.1, s32[1,512]{1,0:T(1,128)} %bitcast.4, f32[1,512]{1,0:T(1,128)} %bitcast.5, f32[1,2048]{1,0:T(1,128)} %bitcast.3, bf16[512,2048]{1,0:T(8,128)(2,1)} %din.1, bf16[2048,512]{1,0:T(8,128)(2,1)} %dout.1, bf16[1,2048,2048]{2,1,0:T(8,128)(2,1)} %ein_h.1, ...), custom_call_target="tpu_custom_call" | custom-call | tf_op jit(solution)/shard_map/pallas_call | solution.py:716
  101.6 1.9 %copy.10 = bf16[512,512]{1,0:T(8,128)(2,1)} copy(bf16[512,512]{1,0:T(8,128)(2,1)} %shard_map.82) | data formatting | bytes 1048576

commit v4 on v3

--- a/solution.py
+++ b/solution.py
@@ -10,9 +10,9 @@
 EARLY = 1
 
 
-def kernel(G, E, Z, cap, nk, SUBS, tokens, route, gate, gain, din, dout, ein_h, eout_h, out,
+def kernel(G, E, Z, cap, nk, SUBS, tokens, route_h, gate_h, gain_h, din, dout, ein_h, eout_h, out,
            win, wout, ein, eout, tok, normed, disp, dispq, arrived, hbuf, pown, psend, po, rpo, pd, rpd,
-           ret, rret, base, pk, turned, eres,
+           ret, rret, base, pk, turned, eres, route, gate, gain,
            loc, own_s, own_r, d1_s, d1_r, dx_s, dx_r, ag_s, ag_r, pq_s, pq_r,
            wx_s, wx_r, wy_s, wy_r, wp_s, wp_r, zo_s, zo_r, zd_s, zd_r, ret_s, ret_r):
     f32, bf16 = jnp.float32, jnp.bfloat16
@@ -51,13 +51,24 @@
 
     my_rows = pl.ds(pl.multiple_of(e * De, De), De)
     locals_ = [
-        pltpu.make_async_copy(tokens, tok, loc.at[0]),
+        pltpu.make_async_copy(route_h, route, loc.at[0]),
         pltpu.make_async_copy(ein_h.at[0], ein, loc.at[1]),
         pltpu.make_async_copy(eout_h.at[0], eout, loc.at[2]),
         pltpu.make_async_copy(din, win.at[my_rows, :], loc.at[3]),
         pltpu.make_async_copy(dout, wout.at[:, my_rows], loc.at[4]),
     ]
-    locals_[0].start()
+    chunks = 4 if T % 256 == 0 else 1
+    loads = []
+    for k in range(chunks):
+        part = pl.ds(k * (T // chunks), T // chunks)
+        loads.append(pltpu.make_async_copy(tokens.at[part, :], tok.at[part, :], loc.at[5 + k]))
+    small = [
+        pltpu.make_async_copy(gain_h, gain, loc.at[9]),
+        pltpu.make_async_copy(gate_h, gate, loc.at[10]),
+        locals_[0],
+    ]
+    for copy in small + loads:
+        copy.start()
 
     barrier = pltpu.get_barrier_semaphore()
     for k in range(1, E):
@@ -95,9 +106,13 @@
         row, n, col, width = block(m, p, s)
         return (din, dout)[m].at[pl.ds(pl.multiple_of(row, n), n), pl.ds(col, width)]
 
-    def x_copy(m, kc, s):
-        return remote(weight_source(m, g, s), weight(m, e, g, s), wx_s.at[m], wx_r.at[m, kc - 1, s],
-                      ee=expert_at(kc, 0))
+    def direct(m, s):
+        return m == 0 and s == SUBS[0] - 1 and s > 0
+
+    def x_copy(m, kc, s, dg=0):
+        half = lax.rem(g - dg + G, G)
+        return remote(weight_source(m, half, s), weight(m, e, half, s), wx_s.at[m],
+                      wx_r.at[m, kc - 1, s + dg], ee=expert_at(kc, 0))
 
     def y_copy(m, kc, s, dg):
         w = weight(m, expert_at(-kc, 0), g, s)
@@ -114,14 +129,15 @@
         while issued[0] < min(upto, len(steps)):
             m, s = steps[issued[0]]
             for kc in range(1, C):
-                x_copy(m, kc, s).start()
+                for dg in range(G if direct(m, s) else 1):
+                    x_copy(m, kc, s, dg).start()
             issued[0] += 1
 
     def relay(upto):
         while relayed[0] < min(upto, taken[0]):
             m, s = steps[relayed[0]]
             for kc in range(1, C):
-                for dg in range(1, G):
+                for dg in range(1, 1 if direct(m, s) else G):
                     y_copy(m, kc, s, dg).wait_recv()
                     p_copy(m, kc, s, dg).start()
             relayed[0] += 1
@@ -130,10 +146,12 @@
         while taken[0] < min(upto, len(steps)):
             m, s = steps[taken[0]]
             for kc in range(1, C):
-                x_copy(m, kc, s).wait_recv()
-                for dg in range(1, G):
+                for dg in range(G if direct(m, s) else 1):
+                    x_copy(m, kc, s, dg).wait_recv()
+                for dg in range(1, 1 if direct(m, s) else G):
                     y_copy(m, kc, s, dg).start()
-                p_copy(m, kc, s, 0).start()
+                for dg in range(G if direct(m, s) else 1):
+                    p_copy(m, kc, s, dg).start()
             taken[0] += 1
 
     def weight_part(m, rows, cols):
@@ -144,9 +162,8 @@
         remote(w, w, wp_s.at[0], wp_r.at[n], ee=partner).wait_recv()
 
     issue(EARLY)
-    locals_[0].wait()
-    for copy in locals_[1:]:
-        copy.start()
+    for copy in small:
+        copy.wait()
 
     nrow = min(64, T)
 
@@ -157,7 +174,12 @@
         normed[rows, :] = (x * lax.rsqrt(ms + 1e-06) * gain[...]).astype(bf16)
         return carry
 
-    lax.fori_loop(0, T // nrow, norm_step, 0)
+    for k in range(chunks):
+        loads[k].wait()
+        if k == chunks - 1:
+            for copy in locals_[1:]:
+                copy.start()
+        lax.fori_loop(k * (T // nrow) // chunks, (k + 1) * (T // nrow) // chunks, norm_step, 0)
 
     picked = route[...]
     lanes = -(-E // 8) * 8
@@ -230,33 +252,35 @@
     def hops(q):
         return Z - 2 if q in fast else Z - 1
 
-    def gather(q, t):
+    def gather(q, t, middle=True, edges=True):
         if t == 0:
             dx_copy(q, 0, z).wait_recv()
-
-        @when(z >= t)
+        inner = (z > 0) & (z < Z - 1)
+        here = True if middle and edges else inner if middle else ~inner
+
+        @when((z >= t) & here)
         def _():
             if t > 0:
                 hop(q, 0, t, z - t).wait_recv()
-        if t < hops(q):
+        if t < hops(q) and middle:
             @when((z >= t) & (z < Z - 1))
             def _():
                 hop(q, 0, t + 1, z - t).start()
 
-        @when(z + t <= Z - 1)
+        @when((z + t <= Z - 1) & here)
         def _():
             if t > 0:
                 hop(q, 1, t, z + t).wait_recv()
-        if t < hops(q):
+        if t < hops(q) and middle:
             @when((z + t <= Z - 1) & (z > 0))
             def _():
                 hop(q, 1, t + 1, z + t).start()
 
-    def hidden(load, rows, w, lo=0, hi=None):
+    def hidden(load, rows, w, lo=0, hi=None, at=0):
         def step(i, carry):
             cols = pl.ds(pl.multiple_of(i * 256, 256), 256)
             acc = jnp.dot(load(), w[:, cols], preferred_element_type=f32)
-            hbuf[0:rows, cols] = jax.nn.gelu(acc).astype(bf16)
+            hbuf[at:at + rows, cols] = jax.nn.gelu(acc).astype(bf16)
             return carry
 
         lax.fori_loop(lo, F // 256 if hi is None else hi, step, 0)
@@ -354,8 +378,8 @@
                 return carry
 
             lax.fori_loop(0, share // 256, step, 0)
-            if i > 0:
-                zo_edge(q, i - 1)
+            if i < Z - 1:
+                zo_edge(q, i)
             if between is not None:
                 between(i)
 
@@ -435,7 +459,7 @@
         if final:
             for k in slow:
                 for t in range(2, Z - 1):
-                    gather(k, t)
+                    gather(k, t, edges=t == 0)
         expert_out(q, (lambda i: take(point(4))) if final else None)
     weights(5, 2)
     pq_copy.wait_recv()
@@ -449,21 +473,25 @@
     lax.fori_loop(0, own_blocks, own_rows, 0)
 
     def serve(i):
+        if i == 0:
+            take(point(8))
         if i == Z // 2 - 1:
             relay(point(5))
             passes(zo_near, fast, 0)
         if i == Z // 2:
-            weights(8, 6)
+            relay(point(6))
 
     for n, q in enumerate(slow):
         final = n == len(slow) - 1
+        for t in range(2, Z - 1):
+            gather(q, t, middle=False)
         gather(q, Z - 1)
         if n == 0:
             weights(6, 3)
         expert_hidden(q, (lambda: weights(7, 4)) if final else None)
         expert_out(q, serve if final else None)
     passes(zo_near, fast, 1)
-    weights(9, 7)
+    relay(point(7))
     passes(zo_far, fast, 0)
     relay(point(8))
     take(point(10))
@@ -471,23 +499,6 @@
     own_copies[0].wait_recv()
     collect(0)
 
-    def mlp_hidden(i):
-        hidden(lambda: normed[...], T, win, *part_of(i, 4))
-
-    mlp_hidden(0)
-    weights(11, 9)
-    mlp_hidden(1)
-    take(point(12))
-    passes(zo_far, fast, 1)
-    for t in range(2, Z - 1):
-        passes(zo_near, fast, t)
-        passes(zo_far, fast, t)
-    mlp_hidden(2)
-    relay(point(10))
-    passes(zo_near, slow, 0)
-    mlp_hidden(3)
-    weights(13, 11)
-
     nr = 2 if T % 32 == 0 else 1
     tall = T // nr
     halves = range(nr)
@@ -497,8 +508,6 @@
         n = c * nr + r
         return remote(pd.at[d, rows, cols], rpd.at[slot, rows, cols], zd_s.at[0], zd_r.at[slot, n], zz=to)
 
-    locals_[4].wait()
-    own_copies[1].wait_recv()
     mine = Z // C if Z % C == 0 else 0
     lined = C == 2 and nk == 2 and mine > 1
     turn = lax.rem(upper + chip, 2)
@@ -509,60 +518,59 @@
             return chip * (Z - 1 - low) + (1 - chip) * low
         return lax.rem(chip * mine + i, Z)
 
-    def late(i, c):
-        return c == nk - 1 and lined and i < mine
-
-    def dense(i, c):
+    def late(i, c, r):
+        return c == nk - 1 and r == nr - 1 and lined and i < mine
+
+    def dense(i, c, group=None):
+        group = halves if group is None else group
         d = slice_number(i)
+        rows = slice(group[0] * tall, (group[-1] + 1) * tall)
         if lined and i < mine:
             d = turn * d + (1 - turn) * slice_number(mine - 1 - i)
 
         def step(k, carry):
             cols = pl.ds(pl.multiple_of(d * share + c * wide + k * tn, tn), tn)
-            acc = jnp.dot(hbuf[0:T, :], wout[:, cols], preferred_element_type=f32)
-            pd[d, :, pl.ds(pl.multiple_of(c * wide + k * tn, tn), tn)] = (acc + eres[:, cols].astype(f32)).astype(bf16)
+            acc = jnp.dot(hbuf[rows, :], wout[:, cols], preferred_element_type=f32)
+            pd[d, rows, pl.ds(pl.multiple_of(c * wide + k * tn, tn), tn)] = (acc + eres[rows, cols].astype(f32)).astype(bf16)
             return carry
 
         lax.fori_loop(0, wide // tn, step, 0)
 
-        dense_edge(i, c, False, d)
-
-    def dense_edge(i, c, again, d):
+        for r in group:
+            dense_edge(i, c, r, False, d)
+
+    def dense_edge(i, c, r, again, d):
         beside = ((z == 0) & (d == 1)) | ((z == Z - 1) & (d == Z - 2))
-        go = (beside if again else ~beside) if late(i, c) else True
-        if again and not late(i, c):
+        go = (beside if again else ~beside) if late(i, c, r) else True
+        if again and not late(i, c, r):
             return
 
         @when((z == 0) & (d > 0) & go)
         def _():
-            for r in halves:
-                zd_copy(d, d, c, r, above).start()
+            zd_copy(d, d, c, r, above).start()
 
         for slot, near in ((d, z > d + 1), (Z, z == d + 1)):
             @when((z == Z - 1) & near & go)
             def _():
-                for r in halves:
-                    zd_copy(d, slot, c, r, below).start()
-
-    def zd_pass(i, c):
+                zd_copy(d, slot, c, r, below).start()
+
+    def zd_pass(i, c, r):
         d = slice_number(i)
-        cols = pl.ds(c * wide, wide)
-        for r in halves:
-            rows = pl.ds(r * tall, tall)
-
-            @when((z > 0) & (z < Z - 1) & (z != d))
+        rows, cols = pl.ds(r * tall, tall), pl.ds(c * wide, wide)
+
+        @when((z > 0) & (z < Z - 1) & (z != d))
+        def _():
+            zd_copy(d, d, c, r, above).wait_recv()
+            pd[d, rows, cols] = (pd[d, rows, cols].astype(f32) + rpd[d, rows, cols].astype(f32)).astype(bf16)
+
+        @when((z > 0) & (z < d))
+        def _():
+            zd_copy(d, d, c, r, above).start()
+
+        for slot, near in ((d, z > d + 1), (Z, z == d + 1)):
+            @when((z < Z - 1) & near)
             def _():
-                zd_copy(d, d, c, r, above).wait_recv()
-                pd[d, rows, cols] = (pd[d, rows, cols].astype(f32) + rpd[d, rows, cols].astype(f32)).astype(bf16)
-
-            @when((z > 0) & (z < d))
-            def _():
-                zd_copy(d, d, c, r, above).start()
-
-            for slot, near in ((d, z > d + 1), (Z, z == d + 1)):
-                @when((z < Z - 1) & near)
-                def _():
-                    zd_copy(d, slot, c, r, below).start()
+                zd_copy(d, slot, c, r, below).start()
 
     trow = min(128, T)
     residual = slice_at(z)
@@ -603,6 +611,9 @@
         for m in range(2):
             for sem, n in ((wx_s, 1), (wy_s, G - 1), (wp_s, G)):
                 rows, cols = ((C - 1) * De // G * n, F) if m == 0 else (F // G * n, (C - 1) * De)
+                if direct(m, SUBS[0] - 1) and sem is not wp_s:
+                    extra = (C - 1) * (G - 1) * De // G // SUBS[0]
+                    rows += extra if sem is wx_s else -extra
                 w = weight_part(m, rows, cols)
                 remote(w, w, sem.at[m], wp_r.at[0], ee=partner).wait_send()
 
@@ -625,10 +636,13 @@
 
     per = SUBS[1] // nk
     def along(kind):
-        for i, c in kind:
-            zd_pass(i, c)
+        for i, c, r in kind:
+            zd_pass(i, c, r)
 
     def in_turn(first_kind, second_kind):
+        if not lined:
+            return
+
         @when(turn == 0)
         def _():
             along(first_kind)
@@ -638,12 +652,50 @@
             along(second_kind)
 
     near, far = list(range(mine, Z)), list(range(mine))
-
-    for i in range(mine):
-        dense(i, 0)
+    n0, n1, f0 = near[0], near[1:], far[0] if far else 0
+
+    def both(items, c):
+        return [(i, c, r) for i in items for r in halves]
+
+    def rest_of(items, c):
+        return [(i, c, r) for i in items for r in halves[1:]]
+
+
+    def mlp_hidden(group, i, n):
+        rows = slice(group[0] * tall, (group[-1] + 1) * tall)
+        hidden(lambda: normed[rows, :], len(group) * tall, win, *part_of(i, n), at=group[0] * tall)
+
+    groups = [halves[:1], halves[1:]] if lined else [halves]
+    mlp_hidden(groups[0], 0, 2)
+    weights(11, 9)
+    mlp_hidden(groups[0], 1, 2)
+    locals_[4].wait()
+    own_copies[1].wait_recv()
+    if lined:
+        dense(0, 0, groups[0])
+        dense(0, 1, groups[0])
+    take(point(12))
+    passes(zo_far, fast, 1)
+    for t in range(2, Z - 1):
+        passes(zo_near, fast, t)
+        passes(zo_far, fast, t)
+    relay(point(10))
+    if lined:
+        mlp_hidden(groups[1], 0, 2)
+        passes(zo_near, slow, 0)
+        mlp_hidden(groups[1], 1, 2)
+        weights(13, 11)
+        dense(0, 0, groups[1])
+        dense(1, 0)
+    else:
+        passes(zo_near, slow, 0)
+        weights(13, 11)
+        for i in range(mine):
+            dense(i, 0)
     weights(14, 12)
     passes(zo_near, slow, 1)
     passes(zo_far, slow, 0)
+    in_turn([], [(f0, 0, 0)])
     if nk > 1:
         collect(1)
         for i in range(mine, Z):
@@ -653,9 +705,10 @@
         for q in fast:
             zo_final(q)
             ret_copy(q).start()
+        in_turn([(n0, 0, 0)], [(f0, 1, 0)] + rest_of([f0], 0))
         for c in range(1, nk):
             for i in range(mine):
-                dense(i, c)
+                dense(i, c, groups[-1] if i == 0 else halves)
     weights(16, 14)
     for t in range(1 if nk == 1 else 2, Z - 1):
         passes(zo_near, slow, t)
@@ -663,29 +716,29 @@
     for q in slow if nk > 1 else units:
         zo_final(q)
         ret_copy(q).start()
-    if lined:
-        in_turn([], [(i, 0) for i in far[:1]])
+    in_turn(rest_of([n0], 0), both(far[1:], 0))
     relay(point(15))
+    in_turn([(i, 0, 0) for i in n1[:1]], [(n0, 0, 0)])
     relay(point(16))
     collect(nk)
     for i in range(mine, Z):
         dense(i, nk - 1)
+        if i == mine:
+            in_turn(rest_of(n1[:1], 0), rest_of([n0], 0))
     for c in range(nk):
         for i in range(Z):
-            dense_edge(i, c, True, slice_number(i))
-    if lined:
-        in_turn([(near[0], 0)], [(i, 0) for i in far[1:]])
-        combine_experts()
-        in_turn([(i, 0) for i in far + near[1:]] + [(near[0], 1)],
-                [(far[0], 1)] + [(i, 0) for i in near] + [(i, 1) for i in far[1:]])
-        sent()
-        in_turn([(i, 1) for i in far + near[1:]], [(i, 1) for i in near])
-    else:
-        for c in range(nk):
-            along([(i, c) for i in range(Z)])
-            if c == 0:
-                combine_experts()
-                sent()
+            for r in halves:
+                dense_edge(i, c, r, True, slice_number(i))
+    in_turn(both(far, 0) + both(n1[1:], 0), both(n1, 0))
+    if not lined:
+        along([(i, 0, r) for i in range(Z) for r in halves])
+    combine_experts()
+    in_turn([(f0, 1, 0), (n0, 1, 0)], rest_of([f0], 1))
+    sent()
+    in_turn(rest_of([n0], 1) + rest_of([f0], 1) + both(far[1:], 1) + both(n1, 1),
+            both(far[1:], 1) + both(near, 1))
+    if not lined:
+        along([(i, c, r) for c in range(1, nk) for i in range(Z) for r in halves])
     for c in range(nk):
         finish(c)
 
@@ -716,7 +769,7 @@
     return pl.pallas_call(
         functools.partial(kernel, G, E, Z, cap, nk, splits),
         out_shape=jax.ShapeDtypeStruct((T, share), bf16),
-        in_specs=[any_, vmem, vmem, vmem, any_, any_, any_, any_],
+        in_specs=[any_, any_, any_, any_, any_, any_, any_, any_],
         out_specs=vmem,
         scratch_shapes=[
             pltpu.VMEM((D, F), bf16), pltpu.VMEM((F, D), bf16),
@@ -730,9 +783,10 @@
             pltpu.VMEM((others, share), bf16), pltpu.VMEM((others, share), bf16),
             pltpu.VMEM((T, share), jnp.float32), pltpu.VMEM((T, 2 * cap), bf16),
             pltpu.VMEM((T, 128), jnp.float32), pltpu.VMEM((T, D), bf16),
-            dma((5,)), dma((2,)), dma((2,)), dma((1,)), dma((1,)), dma((away, 2)), dma((away, 2)),
+            pltpu.VMEM((1, T), jnp.int32), pltpu.VMEM((1, T), jnp.float32), pltpu.VMEM((1, D), jnp.float32),
+            dma((12,)), dma((2,)), dma((2,)), dma((1,)), dma((1,)), dma((away, 2)), dma((away, 2)),
             dma((away, 2, Z - 1)), dma((away, 2, Z - 1)), dma((1,)), dma((1,)),
-            dma((2,)), dma((2, C - 1, subs)), dma((2,)), dma((2, C - 1, subs, G - 1)), dma((2,)), dma((1 + nk,)),
+            dma((2,)), dma((2, C - 1, subs + G - 1)), dma((2,)), dma((2, C - 1, subs, G - 1)), dma((2,)), dma((1 + nk,)),
             dma((1,)), dma((away, Z + 1)), dma((1,)), dma((Z + 1, 2 * nk)), dma((away,)), dma((away,)),
         ],
         compiler_params=pltpu.CompilerParams(

time: 104 us -> 99.1 us (0.953)
  Pallas kernels: 102 us -> 95.8 us
    pallas_call x1, Pallas kernels: 102 us -> 95.8 us  [local(): pl.pallas_call(functools.partial(kernel, G, E, Z, cap, nk, splits), out_s...]
where the time goes in v4:
time: 99.1 us; the launch traced here: 97.6 us
  Pallas kernels  95.8 us (97%)
  local copies, waits for them, and re-layouts  1.87 us (2%)
    pallas_call x1, Pallas kernels, local(): pl.pallas_call(functools.partial(kernel, G, E, Z, cap, nk, splits), out_s...  95.8 us

profile of v4, /device:TPU:2, one launch (start us, length us, event | category | flops | bytes accessed | tf_op | source)
XLA Modules:
  0.0 97.6 jit_solution(9228303401797370934)
XLA Ops:
  0.0 95.8 %shard_map.82 = bf16[512,512]{1,0:T(8,128)(2,1)} custom-call(bf16[512,2048]{1,0:T(8,128)(2,1)} %tokens.1, s32[1,512]{1,0:T(1,128)} %bitcast.4, f32[1,512]{1,0:T(1,128)} %bitcast.5, f32[1,2048]{1,0:T(1,128)} %bitcast.3, bf16[512,2048]{1,0:T(8,128)(2,1)} %din.1, bf16[2048,512]{1,0:T(8,128)(2,1)} %dout.1, bf16[1,2048,2048]{2,1,0:T(8,128)(2,1)} %ein_h.1, ...), custom_call_target="tpu_custom_call" | custom-call | tf_op jit(solution)/shard_map/pallas_call | solution.py:769
  95.8 1.9 %copy.10 = bf16[512,512]{1,0:T(8,128)(2,1)} copy(bf16[512,512]{1,0:T(8,128)(2,1)} %shard_map.82) | data formatting | bytes 1048576

commit v5 on v4

--- a/solution.py
+++ b/solution.py
@@ -7,12 +7,10 @@
 from jax.experimental.pallas import tpu as pltpu
 from jax.sharding import PartitionSpec as P
 
-EARLY = 1
-
 
 def kernel(G, E, Z, cap, nk, SUBS, tokens, route_h, gate_h, gain_h, din, dout, ein_h, eout_h, out,
            win, wout, ein, eout, tok, normed, disp, dispq, arrived, hbuf, pown, psend, po, rpo, pd, rpd,
-           ret, rret, base, pk, turned, eres, route, gate, gain,
+           ret, rret, base, pk, turned, eres, acc, route, gate, gain,
            loc, own_s, own_r, d1_s, d1_r, dx_s, dx_r, ag_s, ag_r, pq_s, pq_r,
            wx_s, wx_r, wy_s, wy_r, wp_s, wp_r, zo_s, zo_r, zd_s, zd_r, ret_s, ret_r):
     f32, bf16 = jnp.float32, jnp.bfloat16
@@ -80,7 +78,6 @@
     for k in range(1, G):
         pl.semaphore_signal(barrier, inc=1, device_id={"groups": lax.rem(g + k, G), "expert": e, "cuts": z},
                             device_id_type=pl.DeviceIdType.MESH)
-    pl.semaphore_wait(barrier, (E - 1) + (Z - 1) + (G - 1))
 
     own_copies = [
         remote(din, win.at[my_rows, :], own_s.at[0], own_r.at[0], ee=partner),
@@ -107,12 +104,15 @@
         return (din, dout)[m].at[pl.ds(pl.multiple_of(row, n), n), pl.ds(col, width)]
 
     def direct(m, s):
-        return m == 0 and s == SUBS[0] - 1 and s > 0
+        per = SUBS[0] if m == 0 else SUBS[1] // nk
+        return per > 1 and s % per == per - 1
 
     def x_copy(m, kc, s, dg=0):
         half = lax.rem(g - dg + G, G)
+        group = s // (SUBS[1] // nk) if m else 0
+        place = s if dg == 0 else max(SUBS) + group * (G - 1) + dg - 1
         return remote(weight_source(m, half, s), weight(m, e, half, s), wx_s.at[m],
-                      wx_r.at[m, kc - 1, s + dg], ee=expert_at(kc, 0))
+                      wx_r.at[m, kc - 1, place], ee=expert_at(kc, 0))
 
     def y_copy(m, kc, s, dg):
         w = weight(m, expert_at(-kc, 0), g, s)
@@ -161,7 +161,6 @@
         w = weight_part(1, F, (C - 1) * De // nk) if n else weight_part(0, (C - 1) * De, F)
         remote(w, w, wp_s.at[0], wp_r.at[n], ee=partner).wait_recv()
 
-    issue(EARLY)
     for copy in small:
         copy.wait()
 
@@ -220,19 +219,16 @@
 
     d1_copy = remote(dispq, arrived.at[pl.ds(cap, cap), :], d1_s.at[0], d1_r.at[0], ee=partner)
 
-    pending = None
     for q in units:
         fill_slice(q, 0, z)
-        if pending is not None:
-            dx_copy(pending, 0, z).start()
-        pending = q
+    pl.semaphore_wait(barrier, (E - 1) + (Z - 1) + (G - 1))
+    for q in units:
+        dx_copy(q, 0, z).start()
     for at, s in ends:
         @when(z == at)
         def _():
             for q in fast:
                 fill_slice(q, 1, s)
-    if pending is not None:
-        dx_copy(pending, 0, z).start()
     fill(1, dispq)
     for at, s in ends:
         @when(z == at)
@@ -279,8 +275,8 @@
     def hidden(load, rows, w, lo=0, hi=None, at=0):
         def step(i, carry):
             cols = pl.ds(pl.multiple_of(i * 256, 256), 256)
-            acc = jnp.dot(load(), w[:, cols], preferred_element_type=f32)
-            hbuf[at:at + rows, cols] = jax.nn.gelu(acc).astype(bf16)
+            product = jnp.dot(load(), w[:, cols], preferred_element_type=f32)
+            hbuf[at:at + rows, cols] = jax.nn.gelu(product).astype(bf16)
             return carry
 
         lax.fori_loop(lo, F // 256 if hi is None else hi, step, 0)
@@ -291,7 +287,6 @@
         return i * blocks // n, (i + 1) * blocks // n
 
     pair = 2 * cap
-    take(EARLY)
     first_row = lax.broadcasted_iota(jnp.int32, (128, T), 0) == 0
     turned[...] = jnp.transpose(jnp.where(first_row, slot_row, gate[...]))
     slot_col = turned[:, 0:1]
@@ -305,8 +300,10 @@
     for i in range(4):
         hidden(lambda: arrived[0:pair, :], pair, ein, *part_of(i, 4))
         if i == 1:
-            for q in units:
+            for q in fast:
                 gather(q, 0)
+    for q in slow:
+        gather(q, 0)
 
     locals_[2].wait()
 
@@ -319,11 +316,49 @@
 
     own_blocks = D // 256
     lax.fori_loop(0, own_blocks // 2, own_step, 0)
+
+    ahead = Z == 4 and len(fast) == 1
+    last_fast, last_slow = lax.rem(z + 2, Z), (Z - 1) * (1 - upper)
+
+    def take_extra(q):
+        for at, s in ends:
+            @when(z == at)
+            def _():
+                dx_copy(q, 1, s).wait_recv()
+
+    def slice_dot(q, s, cols):
+        return jnp.dot(arrived[q * cap:(q + 1) * cap, slice_at(s)], ein[slice_at(s), cols],
+                       preferred_element_type=f32)
+
+    def multiply_ahead(q, last):
+        def step(i, carry):
+            cols = pl.ds(pl.multiple_of(i * 256, 256), 256)
+            acc[:, cols] = sum(slice_dot(q, lax.rem(last + k, Z), cols) for k in range(1, Z))
+            return carry
+
+        lax.fori_loop(0, blocks, step, 0)
+
+    def multiply_last(q, last, at):
+        def step(i, carry):
+            cols = pl.ds(pl.multiple_of(i * 256, 256), 256)
+            hbuf[at:at + cap, cols] = jax.nn.gelu(acc[:, cols] + slice_dot(q, last, cols)).astype(bf16)
+            return carry
+
+        lax.fori_loop(0, blocks, step, 0)
+
     if Z > 2:
-        for q in units:
+        for q in fast:
             gather(q, 1)
-    relay(EARLY)
-    lax.fori_loop(own_blocks // 2, own_blocks, own_step, 0)
+    if ahead:
+        take_extra(fast[0])
+        multiply_ahead(fast[0], last_fast)
+    if Z > 2:
+        for q in slow:
+            gather(q, 1)
+
+    def own_rest():
+        lax.fori_loop(own_blocks // 2, own_blocks, own_step, 0)
+        pq_copy.start()
 
     @when(z == 0)
     def _():
@@ -336,7 +371,8 @@
         rpd[Z] = jnp.zeros(rpd.shape[1:], bf16)
 
     pq_copy = remote(psend, pown.at[pl.ds(cap, cap), :], pq_s.at[0], pq_r.at[0], ee=partner)
-    pq_copy.start()
+    if not ahead:
+        own_rest()
 
     def zo_copy(q, d, slot, to):
         rows = pl.ds((q - 2) * cap, cap)
@@ -356,23 +392,20 @@
 
     def expert_hidden(q, between=None):
         if q in fast:
-            for at, s in ends:
-                @when(z == at)
-                def _():
-                    dx_copy(q, 1, s).wait_recv()
+            take_extra(q)
         rows = slice(q * cap, (q + 1) * cap)
         hidden(lambda: arrived[rows, :], cap, ein, *part_of(0, 2))
         if between is not None:
             between()
         hidden(lambda: arrived[rows, :], cap, ein, *part_of(1, 2))
 
-    def expert_out(q, between=None):
+    def expert_out(q, between=None, at=0):
         rows = slice((q - 2) * cap, (q - 1) * cap)
         for i in range(Z):
             d = (1 - upper) * (Z - 1 - i) + upper * i
 
             def step(k, carry):
-                acc = jnp.dot(hbuf[0:cap, :], eout[:, pl.ds(pl.multiple_of(d * share + k * 256, 256), 256)],
+                acc = jnp.dot(hbuf[at:at + cap, :], eout[:, pl.ds(pl.multiple_of(d * share + k * 256, 256), 256)],
                               preferred_element_type=f32)
                 po[d, rows, pl.ds(pl.multiple_of(k * 256, 256), 256)] = acc.astype(bf16)
                 return carry
@@ -449,20 +482,34 @@
             for q in group:
                 kind(q, t)
 
+    take(point(1))
     for t in range(2, Z - 1):
         for q in fast:
             gather(q, t)
     take(point(2))
-    for n, q in enumerate(fast):
-        final = n == len(fast) - 1
-        expert_hidden(q, (lambda: take(point(3))) if final else None)
-        if final:
-            for k in slow:
-                for t in range(2, Z - 1):
-                    gather(k, t, edges=t == 0)
-        expert_out(q, (lambda i: take(point(4))) if final else None)
+
+    def slow_hops():
+        for k in slow:
+            for t in range(2, Z - 1):
+                gather(k, t, edges=t == 0)
+
+    def serve_fast(i):
+        if i == 0:
+            take(point(3))
+        if i == 1:
+            slow_hops()
+        if i == Z - 1:
+            take(point(4))
+
+    if ahead:
+        multiply_last(fast[0], last_fast, pair)
+        expert_out(fast[0], serve_fast, pair)
+        own_rest()
+    else:
+        for n, q in enumerate(fast):
+            expert_hidden(q)
+            expert_out(q, serve_fast if n == len(fast) - 1 else None)
     weights(5, 2)
-    pq_copy.wait_recv()
 
     def own_rows(i, carry):
         cols = pl.ds(pl.multiple_of(i * 256, 256), 256)
@@ -470,14 +517,11 @@
         eres[:, cols] = (turned[:, 1:2] * res).astype(bf16)
         return carry
 
-    lax.fori_loop(0, own_blocks, own_rows, 0)
+    def serve_hidden():
+        weights(7, 4)
+        passes(zo_near, fast, 0)
 
     def serve(i):
-        if i == 0:
-            take(point(8))
-        if i == Z // 2 - 1:
-            relay(point(5))
-            passes(zo_near, fast, 0)
         if i == Z // 2:
             relay(point(6))
 
@@ -485,19 +529,30 @@
         final = n == len(slow) - 1
         for t in range(2, Z - 1):
             gather(q, t, middle=False)
+        if ahead:
+            multiply_ahead(q, last_slow)
         gather(q, Z - 1)
         if n == 0:
             weights(6, 3)
-        expert_hidden(q, (lambda: weights(7, 4)) if final else None)
+        if ahead:
+            multiply_last(q, last_slow, 0)
+            serve_hidden()
+        else:
+            expert_hidden(q, serve_hidden if final else None)
+        if final:
+            relay(point(5))
         expert_out(q, serve if final else None)
     passes(zo_near, fast, 1)
+    take(point(8))
+    pq_copy.wait_recv()
+    lax.fori_loop(0, own_blocks, own_rows, 0)
     relay(point(7))
     passes(zo_far, fast, 0)
     relay(point(8))
-    take(point(10))
     locals_[3].wait()
     own_copies[0].wait_recv()
     collect(0)
+    take(point(9))
 
     nr = 2 if T % 32 == 0 else 1
     tall = T // nr
@@ -611,8 +666,8 @@
         for m in range(2):
             for sem, n in ((wx_s, 1), (wy_s, G - 1), (wp_s, G)):
                 rows, cols = ((C - 1) * De // G * n, F) if m == 0 else (F // G * n, (C - 1) * De)
-                if direct(m, SUBS[0] - 1) and sem is not wp_s:
-                    extra = (C - 1) * (G - 1) * De // G // SUBS[0]
+                if direct(m, SUBS[m] - 1) and sem is not wp_s:
+                    extra = (C - 1) * (G - 1) * De // G // SUBS[0] if m == 0 else (G - 1) * F // G // (SUBS[1] // nk)
                     rows += extra if sem is wx_s else -extra
                 w = weight_part(m, rows, cols)
                 remote(w, w, sem.at[m], wp_r.at[0], ee=partner).wait_send()
@@ -667,32 +722,33 @@
 
     groups = [halves[:1], halves[1:]] if lined else [halves]
     mlp_hidden(groups[0], 0, 2)
-    weights(11, 9)
+    take(point(10))
     mlp_hidden(groups[0], 1, 2)
     locals_[4].wait()
     own_copies[1].wait_recv()
     if lined:
         dense(0, 0, groups[0])
         dense(0, 1, groups[0])
-    take(point(12))
+    weights(11, 9)
     passes(zo_far, fast, 1)
     for t in range(2, Z - 1):
         passes(zo_near, fast, t)
         passes(zo_far, fast, t)
-    relay(point(10))
     if lined:
         mlp_hidden(groups[1], 0, 2)
+        relay(point(10))
         passes(zo_near, slow, 0)
         mlp_hidden(groups[1], 1, 2)
-        weights(13, 11)
         dense(0, 0, groups[1])
+        weights(12, 11)
         dense(1, 0)
     else:
+        weights(12, 10)
         passes(zo_near, slow, 0)
         weights(13, 11)
         for i in range(mine):
             dense(i, 0)
-    weights(14, 12)
+    relay(point(12))
     passes(zo_near, slow, 1)
     passes(zo_far, slow, 0)
     in_turn([], [(f0, 0, 0)])
@@ -700,7 +756,7 @@
         collect(1)
         for i in range(mine, Z):
             dense(i, 0)
-        weights(15, 13)
+            take(point(13))
         passes(zo_far, slow, 1)
         for q in fast:
             zo_final(q)
@@ -709,7 +765,8 @@
         for c in range(1, nk):
             for i in range(mine):
                 dense(i, c, groups[-1] if i == 0 else halves)
-    weights(16, 14)
+                take(point(14))
+    weights(15, 13)
     for t in range(1 if nk == 1 else 2, Z - 1):
         passes(zo_near, slow, t)
         passes(zo_far, slow, t)
@@ -717,7 +774,8 @@
         zo_final(q)
         ret_copy(q).start()
     in_turn(rest_of([n0], 0), both(far[1:], 0))
-    relay(point(15))
+    relay(point(14))
+    weights(16, 15)
     in_turn([(i, 0, 0) for i in n1[:1]], [(n0, 0, 0)])
     relay(point(16))
     collect(nk)
@@ -776,17 +834,17 @@
             pltpu.VMEM((D, F), bf16), pltpu.VMEM((F, D), bf16),
             pltpu.VMEM((T, D), bf16), pltpu.VMEM((T, D), bf16),
             pltpu.VMEM((2, others, share), bf16), pltpu.VMEM((cap, D), bf16), pltpu.VMEM((E * cap, D), bf16),
-            pltpu.VMEM((max(T, 2 * cap), F), bf16),
+            pltpu.VMEM((max(T, 3 * cap), F), bf16),
             pltpu.VMEM((2 * cap, D), bf16), pltpu.VMEM((cap, D), bf16),
             pltpu.VMEM((Z, others, share), bf16), pltpu.VMEM((Z + 1, others, share), bf16),
             pltpu.VMEM((Z, T, share), bf16), pltpu.VMEM((Z + 1, T, share), bf16),
             pltpu.VMEM((others, share), bf16), pltpu.VMEM((others, share), bf16),
             pltpu.VMEM((T, share), jnp.float32), pltpu.VMEM((T, 2 * cap), bf16),
-            pltpu.VMEM((T, 128), jnp.float32), pltpu.VMEM((T, D), bf16),
+            pltpu.VMEM((T, 128), jnp.float32), pltpu.VMEM((T, D), bf16), pltpu.VMEM((cap, F), jnp.float32),
             pltpu.VMEM((1, T), jnp.int32), pltpu.VMEM((1, T), jnp.float32), pltpu.VMEM((1, D), jnp.float32),
             dma((12,)), dma((2,)), dma((2,)), dma((1,)), dma((1,)), dma((away, 2)), dma((away, 2)),
             dma((away, 2, Z - 1)), dma((away, 2, Z - 1)), dma((1,)), dma((1,)),
-            dma((2,)), dma((2, C - 1, subs + G - 1)), dma((2,)), dma((2, C - 1, subs, G - 1)), dma((2,)), dma((1 + nk,)),
+            dma((2,)), dma((2, C - 1, subs + nk * (G - 1))), dma((2,)), dma((2, C - 1, subs, G - 1)), dma((2,)), dma((1 + nk,)),
             dma((1,)), dma((away, Z + 1)), dma((1,)), dma((Z + 1, 2 * nk)), dma((away,)), dma((away,)),
         ],
         compiler_params=pltpu.CompilerParams(

time: 99.1 us -> 97.3 us (0.982); the launches traced: 97.6 us -> 96.9 us
  no operation moved by 1% of the time
where the time goes in v5:
time: 97.3 us; the launch traced here: 96.9 us
  Pallas kernels  95 us (98%)
  local copies, waits for them, and re-layouts  1.87 us (2%)
    pallas_call x1, Pallas kernels, local(): pl.pallas_call(functools.partial(kernel, G, E, Z, cap, nk, splits), out_s...  95 us

profile of v5, /device:TPU:2, one launch (start us, length us, event | category | flops | bytes accessed | tf_op | source)
XLA Modules:
  0.0 96.9 jit_solution(15479383791743720793)
XLA Ops:
  0.0 95.0 %shard_map.82 = bf16[512,512]{1,0:T(8,128)(2,1)} custom-call(bf16[512,2048]{1,0:T(8,128)(2,1)} %tokens.1, s32[1,512]{1,0:T(1,128)} %bitcast.4, f32[1,512]{1,0:T(1,128)} %bitcast.5, f32[1,2048]{1,0:T(1,128)} %bitcast.3, bf16[512,2048]{1,0:T(8,128)(2,1)} %din.1, bf16[2048,512]{1,0:T(8,128)(2,1)} %dout.1, bf16[1,2048,2048]{2,1,0:T(8,128)(2,1)} %ein_h.1, ...), custom_call_target="tpu_custom_call" | custom-call | tf_op jit(solution)/shard_map/pallas_call | solution.py:827
  95.0 1.9 %copy.10 = bf16[512,512]{1,0:T(8,128)(2,1)} copy(bf16[512,512]{1,0:T(8,128)(2,1)} %shard_map.82) | data formatting | bytes 1048576

commit v6 on v5

--- a/solution.py
+++ b/solution.py
@@ -761,11 +761,12 @@
         for q in fast:
             zo_final(q)
             ret_copy(q).start()
-        in_turn([(n0, 0, 0)], [(f0, 1, 0)] + rest_of([f0], 0))
+        in_turn([], [(f0, 1, 0)] + rest_of([f0], 0))
         for c in range(1, nk):
             for i in range(mine):
                 dense(i, c, groups[-1] if i == 0 else halves)
                 take(point(14))
+    in_turn([(n0, 0, 0)], [])
     weights(15, 13)
     for t in range(1 if nk == 1 else 2, Z - 1):
         passes(zo_near, slow, t)

time: 97.3 us -> 96 us (0.987)
  Pallas kernels: 95 us -> 93.7 us
    pallas_call x1, Pallas kernels: 95 us -> 93.7 us  [local(): pl.pallas_call(functools.partial(kernel, G, E, Z, cap, nk, splits), out_s...]
where the time goes in v6:
time: 96 us; the launch traced here: 95.5 us
  Pallas kernels  93.7 us (98%)
  local copies, waits for them, and re-layouts  1.87 us (2%)
    pallas_call x1, Pallas kernels, local(): pl.pallas_call(functools.partial(kernel, G, E, Z, cap, nk, splits), out_s...  93.7 us

profile of v6, /device:TPU:2, one launch (start us, length us, event | category | flops | bytes accessed | tf_op | source)
XLA Modules:
  0.0 95.5 jit_solution(17918096438928970284)
XLA Ops:
  0.0 93.7 %shard_map.82 = bf16[512,512]{1,0:T(8,128)(2,1)} custom-call(bf16[512,2048]{1,0:T(8,128)(2,1)} %tokens.1, s32[1,512]{1,0:T(1,128)} %bitcast.4, f32[1,512]{1,0:T(1,128)} %bitcast.5, f32[1,2048]{1,0:T(1,128)} %bitcast.3, bf16[512,2048]{1,0:T(8,128)(2,1)} %din.1, bf16[2048,512]{1,0:T(8,128)(2,1)} %dout.1, bf16[1,2048,2048]{2,1,0:T(8,128)(2,1)} %ein_h.1, ...), custom_call_target="tpu_custom_call" | custom-call | tf_op jit(solution)/shard_map/pallas_call | solution.py:828
  93.7 1.9 %copy.10 = bf16[512,512]{1,0:T(8,128)(2,1)} copy(bf16[512,512]{1,0:T(8,128)(2,1)} %shard_map.82) | data formatting | bytes 1048576
